TPU v7x, 32 devices: a whole 2x2x4 slice. The times are simulated.
32 devices in a mesh: ctx: 8 (over y, x, core), fsdp: 4 (over z).
Axes of the slice: x: 2, y: 2, z: 4, core: 2. Of those that a mesh axis runs over, the one named last changes fastest.
Arguments:
- block_input: bfloat16 [4, 1024, 2048], P('fsdp', 'ctx'), may hold values from -6 to 6
- output_grad: bfloat16 [4, 1024, 2048], P('fsdp', 'ctx'), may hold values from -6 to 6
- segment: int32 [4, 1024], P('fsdp'), may hold values from 0 to 3, never falling along the last dimension, each value on 1 to 512 neighbouring positions
- slots: int32 [16], replicated, may hold values from 0 to 15, each once
- ln_gain: bfloat16 [2048], P(('ctx', 'fsdp')), may hold values from 0.5 to 1.5
- ln_bias: bfloat16 [2048], P(('ctx', 'fsdp')), may hold values from -2 to 2
- qkv_w: bfloat16 [2048, 6144], P(('ctx', 'fsdp')), may hold values from -1 to 1
- qkv_b: bfloat16 [6144], P(('ctx', 'fsdp')), may hold values from -0.59765625 to 0.59765625
- dense_w: bfloat16 [2048, 2048], P(('ctx', 'fsdp')), may hold values from -0.5 to 0.5
- dense_b: bfloat16 [2048], P(('ctx', 'fsdp')), may hold values from -2 to 2
- fc1_w: bfloat16 [2048, 8192], P(('ctx', 'fsdp')), may hold values from -0.125 to 0.125
- fc1_b: bfloat16 [8192], P(('ctx', 'fsdp')), may hold values from -2 to 2
- fc2_w: bfloat16 [8192, 2048], P(('ctx', 'fsdp')), may hold values from -0.0625 to 0.0625
- fc2_b: bfloat16 [2048], P(('ctx', 'fsdp')), may hold values from -2 to 2
Outputs:
- block_output: bfloat16 [4, 1024, 2048], P('fsdp', 'ctx')
- input_grad: float32 [4, 1024, 2048], P('fsdp', 'ctx')
- d_ln_gain: float32 [2048], P(('ctx', 'fsdp'))
- d_ln_bias: float32 [2048], P(('ctx', 'fsdp'))
- d_qkv_w: float32 [2048, 6144], P(('ctx', 'fsdp'))
- d_qkv_b: float32 [6144], P(('ctx', 'fsdp'))
- d_dense_w: float32 [2048, 2048], P(('ctx', 'fsdp'))
- d_dense_b: float32 [2048], P(('ctx', 'fsdp'))
- d_fc1_w: float32 [2048, 8192], P(('ctx', 'fsdp'))
- d_fc1_b: float32 [8192], P(('ctx', 'fsdp'))
- d_fc2_w: float32 [8192, 2048], P(('ctx', 'fsdp'))
- d_fc2_b: float32 [2048], P(('ctx', 'fsdp'))
Inputs may be any that keep to these rules, and one draw needn't show every extreme that they name: `segment`: ids never fall along positions; each of the 4 documents of a sequence spans 1 to 512 positions, one exactly that many. `slots`: every stretch number appears exactly once.
All inputs are finite; a program needn't handle non-finite values.
Results may differ from a plain program's by a relative error of at most 0.014.
Values may be sent and summed in bfloat16 or wider, within the bound.
A program may use at most 384 MiB of HBM per device.

v0:
```python
import math

import jax
import jax.numpy as jnp
from jax import lax
from jax.sharding import PartitionSpec as P

HEADS = 32
ROT = 32


EPS = 1e-05
GELU_C = math.sqrt(2.0 / math.pi)
NEG = -1e30


def shifted(block, axis, distance):
    devices = range(lax.axis_size(axis))
    route = [((i - distance) % len(devices), i) for i in devices]
    return lax.ppermute(block, axis, route)


def gelu_pair(upper):
    inner = GELU_C * (upper + 0.044715 * upper * upper * upper)
    tanh_val = jnp.tanh(inner)
    value = 0.5 * upper * (1.0 + tanh_val)
    slope = 0.5 * (1.0 + tanh_val) + 0.5 * upper * (1.0 - tanh_val * tanh_val) * GELU_C * (
        1.0 + 3.0 * 0.044715 * upper * upper
    )
    return (value, slope)


def rotary_tables(positions):
    half = ROT // 2
    freqs = jnp.exp(-(2.0 * jnp.arange(half, dtype=jnp.float32) / ROT) * math.log(10000.0))
    angles = positions.astype(jnp.float32)[:, None] * freqs[None, :]
    return (jnp.cos(angles)[:, None, :], jnp.sin(angles)[:, None, :])


def rotate(tensor, cosine, sine, sign):
    half = ROT // 2
    first = tensor[..., :half]
    second = tensor[..., half:ROT]
    new_first = first * cosine - sign * second * sine
    new_second = second * cosine + sign * first * sine
    return jnp.concatenate([new_first, new_second, tensor[..., ROT:]], axis=-1)


def contract_rows(left, right):
    return lax.dot_general(
        left, right, (((0,), (0,)), ((), ())), preferred_element_type=jnp.float32
    )


def contract_cols(left, right):
    return lax.dot_general(
        left, right, (((1,), (1,)), ((), ())), preferred_element_type=jnp.float32
    )


def own_columns(matrix, cycle_size, shard_count, member):
    count = matrix.shape[0]
    piece_width = matrix.shape[1] // (cycle_size * shard_count)
    parted = matrix.reshape(count, cycle_size, shard_count, piece_width)
    return lax.dynamic_slice_in_dim(parted, member, 1, 2).reshape(count, cycle_size * piece_width)


def per_device(
    block_input,
    output_grad,
    segment,
    slots,
    ln_gain,
    ln_bias,
    qkv_w,
    qkv_b,
    dense_w,
    dense_b,
    fc1_w,
    fc1_b,
    fc2_w,
    fc2_b,
):
    cycle_size = lax.axis_size("ctx")
    index = lax.axis_index("ctx")
    shard_count = lax.axis_size("fsdp")
    member = lax.axis_index("fsdp")
    tokens = block_input.shape[1]
    width = block_input.shape[2]
    stretch = tokens // 2
    heads = HEADS
    head_dim = width // heads
    scale = head_dim ** (-0.5)
    seg_row = segment[0]
    slot_ids = jnp.arange(2 * cycle_size, dtype=jnp.int32)

    def positions(start, count):
        rows = start + jnp.arange(count, dtype=jnp.int32)
        slot = rows // stretch
        owner = jnp.sum(jnp.where(slot[:, None] == slot_ids[None, :], slots[None, :], 0), axis=1)
        return owner * stretch + rows % stretch

    qpos = positions(index * tokens, tokens)
    qdoc = jnp.take(seg_row, qpos)
    cosine, sine = rotary_tables(qpos)
    gain_all, norm_bias_every, w_qkv, b_qkv, w_up, b_up = (
        lax.all_gather(ln_gain, ("ctx", "fsdp"), axis=0, tiled=True),
        lax.all_gather(ln_bias, ("ctx", "fsdp"), axis=0, tiled=True),
        lax.all_gather(qkv_w, ("ctx", "fsdp"), axis=0, tiled=True),
        lax.all_gather(qkv_b, ("ctx", "fsdp"), axis=0, tiled=True),
        lax.all_gather(fc1_w, ("ctx", "fsdp"), axis=0, tiled=True),
        lax.all_gather(fc1_b, ("ctx", "fsdp"), axis=0, tiled=True),
    )
    xf = block_input[0].astype(jnp.float32)
    row_mean = jnp.mean(xf, axis=-1, keepdims=True)
    centered_input = xf - row_mean
    inverse_deviation = lax.rsqrt(
        jnp.mean(centered_input * centered_input, axis=-1, keepdims=True) + EPS
    )
    standardized_input = centered_input * inverse_deviation
    gain_float = gain_all.astype(jnp.float32)
    normed_rows = (standardized_input * gain_float + norm_bias_every.astype(jnp.float32)).astype(
        jnp.bfloat16
    )
    proj = jnp.dot(normed_rows, w_qkv, preferred_element_type=jnp.float32) + b_qkv.astype(
        jnp.float32
    )
    query = rotate(proj[:, :width].reshape(tokens, heads, head_dim), cosine, sine, 1.0).astype(
        jnp.bfloat16
    )
    keys = rotate(
        proj[:, width : 2 * width].reshape(tokens, heads, head_dim), cosine, sine, 1.0
    ).astype(jnp.bfloat16)
    keys_flat = keys.reshape(tokens, width)
    values = proj[:, 2 * width :].astype(jnp.bfloat16)
    acc = jnp.zeros((tokens, heads, head_dim), jnp.float32)
    top = jnp.full((heads, tokens), NEG, jnp.float32)
    key_piece = lax.all_gather(keys_flat, "ctx", axis=0, tiled=True)
    value_piece = lax.all_gather(values, "ctx", axis=0, tiled=True)
    count = key_piece.shape[0]
    kpos = positions(jnp.int32(0), count)
    kdoc = jnp.take(seg_row, kpos)
    mask = ((kpos[None, :] <= qpos[:, None]) & (kdoc[None, :] == qdoc[:, None]))[None]
    scores = (
        jnp.einsum(
            "qhd,khd->hqk",
            query,
            key_piece.reshape(count, heads, head_dim),
            preferred_element_type=jnp.float32,
        )
        * scale
    )
    scores = jnp.where(mask, scores, NEG)
    new_top = jnp.maximum(top, jnp.max(scores, axis=-1))
    factor = jnp.exp(top - new_top)
    expo = jnp.where(mask, jnp.exp(scores - new_top[..., None]), 0.0)
    total = jnp.sum(expo, axis=-1)
    part_sum = jnp.einsum(
        "hqk,khd->qhd",
        expo.astype(jnp.bfloat16),
        value_piece.reshape(count, heads, head_dim),
        preferred_element_type=jnp.float32,
    )
    acc = acc * factor.T[:, :, None] + part_sum
    acc, top, total = (acc, new_top, total)
    attn_heads = (acc / total.T[:, :, None]).astype(jnp.bfloat16)
    lse = top + jnp.log(total)
    attn = attn_heads.reshape(tokens, width)
    w_dense, b_dense, w_down, b_down = (
        lax.all_gather(dense_w, ("ctx", "fsdp"), axis=0, tiled=True),
        lax.all_gather(dense_b, ("ctx", "fsdp"), axis=0, tiled=True),
        lax.all_gather(fc2_w, ("ctx", "fsdp"), axis=0, tiled=True),
        lax.all_gather(fc2_b, ("ctx", "fsdp"), axis=0, tiled=True),
    )
    upper = jnp.dot(normed_rows, w_up, preferred_element_type=jnp.float32) + b_up.astype(
        jnp.float32
    )
    act_f, slope = gelu_pair(upper)
    act = act_f.astype(jnp.bfloat16)
    y_rows = (
        xf
        + jnp.dot(attn, w_dense, preferred_element_type=jnp.float32)
        + b_dense.astype(jnp.float32)
    )
    y_rows = (
        y_rows
        + jnp.dot(act, w_down, preferred_element_type=jnp.float32)
        + b_down.astype(jnp.float32)
    )
    grad_rows = output_grad[0]
    gradient_float = grad_rows.astype(jnp.float32)
    group_attn, group_act, group_grad = (
        lax.all_gather(attn, "fsdp", axis=0, tiled=True),
        lax.all_gather(act, "fsdp", axis=0, tiled=True),
        lax.all_gather(grad_rows, "fsdp", axis=0, tiled=True),
    )
    group_bias = jnp.sum(group_grad.astype(jnp.float32), axis=0)
    own_bias = own_columns(group_bias[None], cycle_size, shard_count, member)[0]
    dense_part = contract_rows(own_columns(group_attn, cycle_size, shard_count, member), group_grad)
    down_part = contract_rows(own_columns(group_act, cycle_size, shard_count, member), group_grad)
    g_dense_w, g_dense_b, g_fc2_w, g_fc2_b = (
        lax.psum_scatter(
            dense_part.astype(jnp.bfloat16), "ctx", scatter_dimension=0, tiled=True
        ).astype(jnp.float32),
        lax.psum_scatter(
            own_bias.astype(jnp.bfloat16), "ctx", scatter_dimension=0, tiled=True
        ).astype(jnp.float32),
        lax.psum_scatter(
            down_part.astype(jnp.bfloat16), "ctx", scatter_dimension=0, tiled=True
        ).astype(jnp.float32),
        lax.psum_scatter(
            own_bias.astype(jnp.bfloat16), "ctx", scatter_dimension=0, tiled=True
        ).astype(jnp.float32),
    )
    dup = contract_cols(grad_rows, w_down) * slope
    up_bias_grad = jnp.sum(dup, axis=0)
    dup_b = dup.astype(jnp.bfloat16)
    dattn = contract_cols(grad_rows, w_dense).astype(jnp.bfloat16).reshape(tokens, heads, head_dim)
    delta = jnp.sum(dattn.astype(jnp.float32) * attn_heads.astype(jnp.float32), axis=-1).T

    def cycle_step(step, carry):
        key_cur, value_cur, dkey_acc, dvalue_acc, dquery_acc = carry
        anchor = (index - step + cycle_size) % cycle_size
        kpos = positions(anchor * tokens, tokens)
        kdoc = jnp.take(seg_row, kpos)
        mask = ((kpos[None, :] <= qpos[:, None]) & (kdoc[None, :] == qdoc[:, None]))[None]
        key_heads = key_cur.reshape(tokens, heads, head_dim)
        scores = (
            jnp.einsum("qhd,khd->hqk", query, key_heads, preferred_element_type=jnp.float32) * scale
        )
        probs = jnp.where(mask, jnp.exp(jnp.where(mask, scores, NEG) - lse[..., None]), 0.0)
        dvalue_acc = dvalue_acc + jnp.einsum(
            "hqk,qhd->khd", probs.astype(jnp.bfloat16), dattn, preferred_element_type=jnp.float32
        ).reshape(tokens, width)
        dprob = jnp.einsum(
            "qhd,khd->hqk",
            dattn,
            value_cur.reshape(tokens, heads, head_dim),
            preferred_element_type=jnp.float32,
        )
        dscore = (probs * (dprob - delta[..., None]) * scale).astype(jnp.bfloat16)
        dquery_acc = dquery_acc + jnp.einsum(
            "hqk,khd->qhd", dscore, key_heads, preferred_element_type=jnp.float32
        )
        dkey_acc = dkey_acc + jnp.einsum(
            "hqk,qhd->khd", dscore, query, preferred_element_type=jnp.float32
        ).reshape(tokens, width)
        key_cur, value_cur = shifted((key_cur, value_cur), "ctx", 1)
        dkey_acc, dvalue_acc = (
            shifted(dkey_acc.astype(jnp.bfloat16), "ctx", 1).astype(dkey_acc.dtype),
            shifted(dvalue_acc.astype(jnp.bfloat16), "ctx", 1).astype(dvalue_acc.dtype),
        )
        return (key_cur, value_cur, dkey_acc, dvalue_acc, dquery_acc)

    flat_zero = jnp.zeros((tokens, width), jnp.float32)
    cycle_init = (
        keys_flat,
        values,
        flat_zero,
        flat_zero,
        jnp.zeros((tokens, heads, head_dim), jnp.float32),
    )
    cycle_out = lax.fori_loop(0, cycle_size, cycle_step, cycle_init)
    dkey_sum, dvalue_sum, dquery_sum = (cycle_out[2], cycle_out[3], cycle_out[4])
    dquery = rotate(dquery_sum, cosine, sine, -1.0).reshape(tokens, width)
    dkey = rotate(dkey_sum.reshape(tokens, heads, head_dim), cosine, sine, -1.0).reshape(
        tokens, width
    )
    dproj = jnp.concatenate([dquery, dkey, dvalue_sum], axis=1)
    qkv_bias_grad = jnp.sum(dproj, axis=0)
    dproj_b = dproj.astype(jnp.bfloat16)
    normed_input_grad = contract_cols(dproj_b, w_qkv) + contract_cols(dup_b, w_up)
    gain_gradient = jnp.sum(normed_input_grad * standardized_input, axis=0)
    lnb_grad = jnp.sum(normed_input_grad, axis=0)
    scaled_rows = normed_input_grad * gain_float
    dx_rows = gradient_float + inverse_deviation * (
        scaled_rows
        - jnp.mean(scaled_rows, axis=-1, keepdims=True)
        - standardized_input * jnp.mean(scaled_rows * standardized_input, axis=-1, keepdims=True)
    )
    group_normed, group_dproj, group_dup = (
        lax.all_gather(normed_rows, "fsdp", axis=0, tiled=True),
        lax.all_gather(dproj_b, "fsdp", axis=0, tiled=True),
        lax.all_gather(dup_b, "fsdp", axis=0, tiled=True),
    )
    own_normed = own_columns(group_normed, cycle_size, shard_count, member)
    g_qkv_w, g_fc1_w = (
        lax.psum_scatter(
            contract_rows(own_normed, group_dproj).astype(jnp.bfloat16),
            "ctx",
            scatter_dimension=0,
            tiled=True,
        ).astype(jnp.float32),
        lax.psum_scatter(
            contract_rows(own_normed, group_dup).astype(jnp.bfloat16),
            "ctx",
            scatter_dimension=0,
            tiled=True,
        ).astype(jnp.float32),
    )
    layer_gain_grad, g_lnb, g_qkv_b, g_fc1_b = (
        lax.psum_scatter(gain_gradient, ("ctx", "fsdp"), scatter_dimension=0, tiled=True),
        lax.psum_scatter(lnb_grad, ("ctx", "fsdp"), scatter_dimension=0, tiled=True),
        lax.psum_scatter(qkv_bias_grad, ("ctx", "fsdp"), scatter_dimension=0, tiled=True),
        lax.psum_scatter(up_bias_grad, ("ctx", "fsdp"), scatter_dimension=0, tiled=True),
    )
    return (
        y_rows.astype(jnp.bfloat16)[None],
        dx_rows[None],
        layer_gain_grad,
        g_lnb,
        g_qkv_w,
        g_qkv_b,
        g_dense_w,
        g_dense_b,
        g_fc1_w,
        g_fc1_b,
        g_fc2_w,
        g_fc2_b,
    )


def solution(mesh):
    in_specs = (
        P("fsdp", "ctx", None),
        P("fsdp", "ctx", None),
        P("fsdp", None),
        P(),
        P(("ctx", "fsdp")),
        P(("ctx", "fsdp")),
        P(("ctx", "fsdp"), None),
        P(("ctx", "fsdp")),
        P(("ctx", "fsdp"), None),
        P(("ctx", "fsdp")),
        P(("ctx", "fsdp"), None),
        P(("ctx", "fsdp")),
        P(("ctx", "fsdp"), None),
        P(("ctx", "fsdp")),
    )
    out_specs = (
        P("fsdp", "ctx", None),
        P("fsdp", "ctx", None),
        P(("ctx", "fsdp")),
        P(("ctx", "fsdp")),
        P(("ctx", "fsdp"), None),
        P(("ctx", "fsdp")),
        P(("ctx", "fsdp"), None),
        P(("ctx", "fsdp")),
        P(("ctx", "fsdp"), None),
        P(("ctx", "fsdp")),
        P(("ctx", "fsdp"), None),
        P(("ctx", "fsdp")),
    )
    return jax.shard_map(
        per_device, mesh=mesh, in_specs=in_specs, out_specs=out_specs, check_vma=False
    )
```

profile of v0, /device:TPU:8, one launch (start us, length us, event | category | flops | bytes accessed | tf_op | source)
XLA Modules:
  0.0 1740.4 jit_solution(4601442492112934153)
XLA Ops:
  13.0 43.1 %all-reduce.11 = (bf16[2048]{0:T(1024)(128)(2,1)S(1)}, bf16[2048]{0:T(1024)(128)(2,1)S(1)}, bf16[6144]{0:T(1024)(128)(2,1)S(1)}, bf16[2048]{0:T(1024)(128)(2,1)}, bf16[2048]{0:T(1024)(128)(2,1)}) all-reduce(bf16[2048]{0:T(1024)(128)(2,1)S(1)} %dynamic-update-slice.1, ...), channel_id=1, replica_groups=mesh['ctx'=8,'fsdp'=4] {'ctx','fsdp'}, use_global_device_ids=true, to_apply=%add.1 | all-reduce | flops 14336 | bytes 57344
  63.4 102.6 %all-gather.15.cloned.1.call-done = bf16[2048,6144]{1,0:T(8,128)(2,1)} async-done(((bf16[64,6144]{1,0:T(8,128)(2,1)}), bf16[2048,6144]{1,0:T(8,128)(2,1)}) %all-gather.15.cloned.1.call-update) | async-done | bytes 25165840 | tf_op jit(solution)/shard_map/all_gather | solution.py:109
  194.3 51.6 %all-gather.21.cloned.1.call-done = bf16[2048,2048]{1,0:T(8,128)(2,1)} async-done(((bf16[64,2048]{1,0:T(8,128)(2,1)}), bf16[2048,2048]{1,0:T(8,128)(2,1)}) %all-gather.21.cloned.1.call-update) | async-done | bytes 8388624 | tf_op jit(solution)/shard_map/all_gather | solution.py:170
  253.6 30.7 %all-gather.17.cloned.1.call-done = bf16[1024,2048]{0,1:T(8,128)(2,1)} async-done(((bf16[128,2048]{0,1:T(8,128)(2,1)}), bf16[1024,2048]{0,1:T(8,128)(2,1)}) %all-gather.17.cloned.1.call-update) | async-done | bytes 4194320 | tf_op jit(solution)/shard_map/all_gather | solution.py:138
  295.5 27.8 %all-gather.19.cloned.1.call-done = bf16[1024,2048]{1,0:T(8,128)(2,1)} async-done(((bf16[128,2048]{1,0:T(8,128)(2,1)}), bf16[1024,2048]{1,0:T(8,128)(2,1)}) %all-gather.19.cloned.1.call-update) | async-done | bytes 4194320 | tf_op jit(solution)/shard_map/all_gather | solution.py:139
  351.5 421.6 %while.25 = (s32[]{:T(128)}, bf16[128,2048]{0,1:T(8,128)(2,1)S(1)}, bf16[128,2048]{0,1:T(8,128)(2,1)}, f32[128,2048]{0,1:T(8,128)}, f32[128,2048]{0,1:T(8,128)},...) while((s32[]{:T(128)}, bf16[128,2048]{0,1:T(8,128)(2,1)S(1)}, ...), condition=%wide.region_9.11_spmd.clone, body=%wide.region_7.10_spmd.clone.sunk | while | flops 342945664 | bytes 44643436 | solution.py:263
  387.4 14.7 collective-permute-done
  456.7 17.0 collective-permute-done.1
  504.9 14.8 collective-permute-done.3
  687.8 14.8 collective-permute-done.3
  704.6 14.7 collective-permute-done
  719.3 17.0 collective-permute-done.1
  778.4 66.7 %all-gather.1 = bf16[32,1,256]{2,1,0:T(2,128)(2,1)S(1)} all-gather(bf16[1,1,256]{2,1,0:T(2,128)(2,1)S(1)} %reshape.541), channel_id=1, replica_groups=mesh['ctx'=8,'fsdp'=4] {'ctx','fsdp'}, dimensions={0}, use_global_device_ids=true | all-gather | bytes 16896 | tf_op jit(solution)/shard_map/all_gather | solution.py:112
  845.1 16.7 multiply_convert_fusion.1
  861.8 19.5 %fusion.69 = (f32[8192]{0:T(1024)}, bf16[128,8192]{1,0:T(8,128)(2,1)}) fusion(f32[128,8192]{1,0:T(8,128)} %get-tuple-element.642, bf16[8192,2048]{1,0:T(8,128)(2,1)} %all-gather.25.cloned.1.call-done, bf16[1,128,2048]{2,1,0:T(8,128)(2,1)} %param.19), kind=kOutput, calls=%fused_computation.157 | convolution fusion | flops 4315930624 | bytes 40402944 | tf_op jit(solution)/shard_map/dot_general | solution.py:56
  890.6 35.5 %all-gather.37.cloned.1.call-done = bf16[1,512,2048]{2,1,0:T(8,128)(2,1)} async-done(((bf16[1,128,2048]{2,1,0:T(8,128)(2,1)}), bf16[1,512,2048]{2,1,0:T(8,128)(2,1)}) %all-gather.37.cloned.1.call-update) | async-done | bytes 2097168 | tf_op jit(solution)/shard_map/all_gather | solution.py:195
  944.2 17.4 fusion.47
  961.7 78.5 %all-gather.29.cloned.1.call-done = bf16[512,6144]{0,1:T(8,128)(2,1)} async-done(((bf16[128,6144]{0,1:T(8,128)(2,1)}), bf16[512,6144]{0,1:T(8,128)(2,1)}) %all-gather.29.cloned.1.call-update) | async-done | bytes 6291472 | tf_op jit(solution)/shard_map/all_gather | solution.py:283
  1048.3 141.8 %all-gather.33.cloned.1.call-done = bf16[512,8192]{1,0:T(8,128)(2,1)} async-done(((bf16[128,8192]{1,0:T(8,128)(2,1)}), bf16[512,8192]{1,0:T(8,128)(2,1)}) %all-gather.33.cloned.1.call-update) | async-done | bytes 8388624 | tf_op jit(solution)/shard_map/all_gather | solution.py:284
  1200.6 139.3 %all-gather.35.cloned.1.call-done = bf16[512,8192]{1,0:T(8,128)(2,1)} async-done(((bf16[128,8192]{1,0:T(8,128)(2,1)}), bf16[512,8192]{1,0:T(8,128)(2,1)}) %all-gather.35.cloned.1.call-update) | async-done | bytes 8388624 | tf_op jit(solution)/shard_map/all_gather | solution.py:194
  1425.4 90.4 %all-reduce.14.cloned.1.call-done = (f32[2048]{0:T(1024)}, f32[2048]{0:T(1024)}, f32[6144]{0:T(1024)}, f32[8192]{0:T(1024)}) async-done(((f32[2048]{0:T(1024)}, f32[2048]{0:T(1024)}, f32[6144]{0:T(1024)}, f32[8192]{0:T(1024)}), (f32[2048]{0:T(1024)}, f32[2048]{0:T(1024)}, f32[6144]{0:T(1024)}, f32[8192]{0:T(1024)})) %all-reduce.14.cloned.1.call-update) | async-done | bytes 73744
  1520.9 59.8 %reduce-scatter.5.cloned.1.call-done = bf16[64,6144]{1,0:T(8,128)(2,1)} async-done(((bf16[512,6144]{1,0:T(8,128)(2,1)}), bf16[64,6144]{1,0:T(8,128)(2,1)}) %reduce-scatter.5.cloned.1.call-update) | async-done | bytes 786448 | tf_op jit(solution)/shard_map/reduce_scatter | solution.py:288
  1583.0 72.5 %reduce-scatter.9.cloned.1.call-done = bf16[64,8192]{1,0:T(8,128)(2,1)} async-done(((bf16[512,8192]{1,0:T(8,128)(2,1)}), bf16[64,8192]{1,0:T(8,128)(2,1)}) %reduce-scatter.9.cloned.1.call-update) | async-done | bytes 1048592 | tf_op jit(solution)/shard_map/reduce_scatter | solution.py:294
  1658.2 72.2 %reduce-scatter.11.cloned.1.call-done = bf16[256,2048]{1,0:T(8,128)(2,1)} async-done(((bf16[2048,2048]{1,0:T(8,128)(2,1)}), bf16[256,2048]{1,0:T(8,128)(2,1)}) %reduce-scatter.11.cloned.1.call-update) | async-done | bytes 1048592 | tf_op jit(solution)/shard_map/reduce_scatter | solution.py:208
  (405 shorter events, 565.9 us)
Async XLA Ops:
  7.2 158.8 %all-gather.15.cloned.1.call-start = ((), (), s32[]{:S(2)}) async-start(), calls=%async_computation.4 | async-start | bytes 25952256 | tf_op jit(solution)/shard_map/all_gather | solution.py:109
  7.9 238.0 %all-gather.21.cloned.1.call-start = ((), (), s32[]{:S(2)}) async-start(), calls=%async_computation.7 | async-start | bytes 8650752 | tf_op jit(solution)/shard_map/all_gather | solution.py:170
  8.7 275.7 %all-gather.17.cloned.1.call-start = ((), (), s32[]{:S(2)}) async-start(), calls=%async_computation.5 | async-start | bytes 4718592 | tf_op jit(solution)/shard_map/all_gather | solution.py:138
  186.0 137.3 %all-gather.19.cloned.1.call-start = ((), (), s32[]{:S(2)}) async-start(), calls=%async_computation.6 | async-start | bytes 4718592 | tf_op jit(solution)/shard_map/all_gather | solution.py:139
  187.0 658.2 %all-gather.23.cloned.1.call-start = ((), (), s32[]{:S(2)}) async-start(), calls=%async_computation.8 | async-start | bytes 34603008 | tf_op jit(solution)/shard_map/all_gather | solution.py:111
  187.6 674.3 %all-gather.25.cloned.1.call-start = ((), (), s32[]{:S(2)}) async-start(), calls=%async_computation.9 | async-start | bytes 34603008 | tf_op jit(solution)/shard_map/all_gather | solution.py:172
  188.1 694.0 %all-gather.27.cloned.1.call-start = ((), (), s32[]{:S(2)}) async-start(), calls=%async_computation.10 | async-start | bytes 2621440 | tf_op jit(solution)/shard_map/all_gather | solution.py:282
  188.9 700.6 %all-gather.31.cloned.1.call-start = ((), (), s32[]{:S(2)}) async-start(), calls=%async_computation.13 | async-start | bytes 2621440 | tf_op jit(solution)/shard_map/all_gather | solution.py:193
  348.6 577.5 %all-gather.37.cloned.1.call-start = ((), (), s32[]{:S(2)}) async-start(), calls=%async_computation.19 | async-start | bytes 2621440 | tf_op jit(solution)/shard_map/all_gather | solution.py:195
  349.4 690.7 %all-gather.29.cloned.1.call-start = ((), (), s32[]{:S(2)}) async-start(), calls=%async_computation.11 | async-start | bytes 7864320 | tf_op jit(solution)/shard_map/all_gather | solution.py:283
  362.7 53.4 %collective-permute-start.1 = (bf16[128,2048]{0,1:T(8,128)(2,1)S(1)}, bf16[128,2048]{0,1:T(8,128)(2,1)}, u32[]{:S(2)}, u32[]{:S(2)}) collective-permute-start(bf16[128,2048]{0,1:T(8,128)(2,1)S(1)} %copy.79), channel_id=1, source_target_pairs={{28,0},{0,4},{4,8},{8,12},{12,16},{16,20},{20,24},{24,28},{29,1},{... | collective-permute-start | bytes 1572872 | tf_op jit(solution)/shard_map/while/body/eval_jaxpr/ppermute | solution.py:20
  426.1 47.5 %collective-permute-start.1 = (bf16[128,2048]{0,1:T(8,128)(2,1)S(1)}, bf16[128,2048]{0,1:T(8,128)(2,1)}, u32[]{:S(2)}, u32[]{:S(2)}) collective-permute-start(bf16[128,2048]{0,1:T(8,128)(2,1)S(1)} %copy.79), channel_id=1, source_target_pairs={{28,0},{0,4},{4,8},{8,12},{12,16},{16,20},{20,24},{24,28},{29,1},{... | collective-permute-start | bytes 1572872 | tf_op jit(solution)/shard_map/while/body/eval_jaxpr/ppermute | solution.py:20
  483.0 44.4 %collective-permute-start = (bf16[128,2048]{0,1:T(8,128)(2,1)S(1)}, bf16[128,2048]{0,1:T(8,128)(2,1)S(1)}, u32[]{:S(2)}, u32[]{:S(2)}) collective-permute-start(bf16[128,2048]{0,1:T(8,128)(2,1)S(1)} %copy.78), channel_id=1, source_target_pairs={{28,0},{0,4},{4,8},{8,12},{12,16},{16,20},{20,24},{24,28},{29,1},{... | collective-permute-start | bytes 1572872 | tf_op jit(solution)/shard_map/while/body/eval_jaxpr/ppermute | solution.py:20
  483.8 49.3 %collective-permute-start.1 = (bf16[128,2048]{0,1:T(8,128)(2,1)S(1)}, bf16[128,2048]{0,1:T(8,128)(2,1)}, u32[]{:S(2)}, u32[]{:S(2)}) collective-permute-start(bf16[128,2048]{0,1:T(8,128)(2,1)S(1)} %copy.79), channel_id=1, source_target_pairs={{28,0},{0,4},{4,8},{8,12},{12,16},{16,20},{20,24},{24,28},{29,1},{... | collective-permute-start | bytes 1572872 | tf_op jit(solution)/shard_map/while/body/eval_jaxpr/ppermute | solution.py:20
  612.8 44.0 %collective-permute-start.1 = (bf16[128,2048]{0,1:T(8,128)(2,1)S(1)}, bf16[128,2048]{0,1:T(8,128)(2,1)}, u32[]{:S(2)}, u32[]{:S(2)}) collective-permute-start(bf16[128,2048]{0,1:T(8,128)(2,1)S(1)} %copy.79), channel_id=1, source_target_pairs={{28,0},{0,4},{4,8},{8,12},{12,16},{16,20},{20,24},{24,28},{29,1},{... | collective-permute-start | bytes 1572872 | tf_op jit(solution)/shard_map/while/body/eval_jaxpr/ppermute | solution.py:20
  666.2 53.1 %collective-permute-start = (bf16[128,2048]{0,1:T(8,128)(2,1)S(1)}, bf16[128,2048]{0,1:T(8,128)(2,1)S(1)}, u32[]{:S(2)}, u32[]{:S(2)}) collective-permute-start(bf16[128,2048]{0,1:T(8,128)(2,1)S(1)} %copy.78), channel_id=1, source_target_pairs={{28,0},{0,4},{4,8},{8,12},{12,16},{16,20},{20,24},{24,28},{29,1},{... | collective-permute-start | bytes 1572872 | tf_op jit(solution)/shard_map/while/body/eval_jaxpr/ppermute | solution.py:20
  666.2 70.1 %collective-permute-start.1 = (bf16[128,2048]{0,1:T(8,128)(2,1)S(1)}, bf16[128,2048]{0,1:T(8,128)(2,1)}, u32[]{:S(2)}, u32[]{:S(2)}) collective-permute-start(bf16[128,2048]{0,1:T(8,128)(2,1)S(1)} %copy.79), channel_id=1, source_target_pairs={{28,0},{0,4},{4,8},{8,12},{12,16},{16,20},{20,24},{24,28},{29,1},{... | collective-permute-start | bytes 1572872 | tf_op jit(solution)/shard_map/while/body/eval_jaxpr/ppermute | solution.py:20
  778.3 411.8 %all-gather.33.cloned.1.call-start = ((), (), s32[]{:S(2)}) async-start(), calls=%async_computation.15 | async-start | bytes 10485760 | tf_op jit(solution)/shard_map/all_gather | solution.py:284
  881.3 458.6 %all-gather.35.cloned.1.call-start = ((), (), s32[]{:S(2)}) async-start(), calls=%async_computation.17 | async-start | bytes 10485760 | tf_op jit(solution)/shard_map/all_gather | solution.py:194
  881.9 526.1 %reduce-scatter.7.cloned.1.call-start = ((), (), s32[]{:S(2)}) async-start(), calls=%async_computation.14 | async-start | bytes 2359296 | tf_op jit(solution)/shard_map/reduce_scatter | solution.py:202
  930.4 585.3 %all-reduce.14.cloned.1.call-start = ((), (), s32[]{:S(2)}) async-start(), calls=%async_computation.20 | async-start | bytes 147456
  961.6 619.1 %reduce-scatter.5.cloned.1.call-start = ((), (), s32[]{:S(2)}) async-start(), calls=%async_computation.12 | async-start | bytes 7077888 | tf_op jit(solution)/shard_map/reduce_scatter | solution.py:288
  1048.3 607.2 %reduce-scatter.9.cloned.1.call-start = ((), (), s32[]{:S(2)}) async-start(), calls=%async_computation.16 | async-start | bytes 9437184 | tf_op jit(solution)/shard_map/reduce_scatter | solution.py:294
  1200.2 530.1 %reduce-scatter.11.cloned.1.call-start = ((), (), s32[]{:S(2)}) async-start(), calls=%async_computation.18 | async-start | bytes 9437184 | tf_op jit(solution)/shard_map/reduce_scatter | solution.py:208
  (58 other events, 1167.0 us)
Sparse Core Ops, SparseCore 0:
  10.9 155.0 all-gather.14
  168.9 76.9 all-gather.20
  248.4 35.9 all-gather.16
  286.7 36.5 all-gather.18
  326.1 232.5 all-gather.22
  561.4 224.4 all-gather.24
  788.1 45.9 all-gather.26
  835.6 43.3 all-gather.30
  880.6 45.4 all-gather.36
  928.1 111.9 all-gather.28
  1042.3 147.7 all-gather.32
  1192.1 147.7 all-gather.34
  1343.2 42.2 reduce-scatter.6
  1391.5 124.1 all-reduce.13
  1519.0 61.6 reduce-scatter.4
  1584.0 71.4 reduce-scatter.8
  1658.8 71.4 reduce-scatter.10
where the time goes:
time: 1750 us; the launch traced here: 1740 us
  waiting for transfers between devices  1170 us (67%)
  matrix products  220 us (13%)
  blocking collectives  124 us (7%)
  local copies, waits for them, and re-layouts  95.9 us (5%)
  other arithmetic  86.3 us (5%)
  starting transfers between devices  24.6 us (1%)
    ppermute x32, waiting for transfers between devices, shifted(): return lax.ppermute(block, axis, route)  267 us
    all_gather x1, waiting for transfers between devices, per_device(): lax.all_gather(dup_b, 'fsdp', axis=0, tiled=True)  142 us
    all_gather x1, waiting for transfers between devices, per_device(): lax.all_gather(act, 'fsdp', axis=0, tiled=True)  139 us
    all_gather x1, waiting for transfers between devices, per_device(): lax.all_gather(qkv_w, ('ctx', 'fsdp'), axis=0, tiled=True)  103 us
    unnamed x18, waiting for transfers between devices  94.9 us
    all_gather x1, waiting for transfers between devices, per_device(): lax.all_gather(dproj_b, 'fsdp', axis=0, tiled=True)  78.5 us
    reduce_scatter x1, waiting for transfers between devices, per_device(): lax.psum_scatter(contract_rows(own_normed, group_dup).astype(jnp.bfloat16...  72.5 us
    reduce_scatter x1, waiting for transfers between devices, per_device(): lax.psum_scatter(down_part.astype(jnp.bfloat16), 'ctx', scatter_dimension...  72.2 us
  transfers between devices with their start and end apart: 49, of which 44 were waited for; matrix products, arithmetic and copies ran while one was open for 23% of the time, Pallas kernels for 0%

commit v1 on v0

--- a/solution.py
+++ b/solution.py
@@ -3,6 +3,8 @@
 import jax
 import jax.numpy as jnp
 from jax import lax
+from jax.experimental import pallas as pl
+from jax.experimental.pallas import tpu as pltpu
 from jax.sharding import PartitionSpec as P
 
 HEADS = 32
@@ -320,6 +322,720 @@
     )
 
 
+BF = jnp.bfloat16
+F32 = jnp.float32
+MESH = pl.DeviceIdType.MESH
+HBM = pl.BlockSpec(memory_space=pl.ANY)
+VM = pl.BlockSpec(memory_space=pltpu.VMEM)
+DMA = pltpu.SemaphoreType.DMA
+VLIM = 60 * 1024 * 1024
+
+
+def place():
+    ctx, z = lax.axis_index("ctx"), lax.axis_index("fsdp")
+    return ctx, lax.div(ctx, 4), lax.rem(lax.div(ctx, 2), 2), lax.rem(ctx, 2), z
+
+
+class Net:
+    def __init__(self):
+        self.ctx, self.y, self.x, self.c, self.z = place()
+        self.yb, self.xb, self.cb = 1 - self.y, 1 - self.x, 1 - self.c
+        self.m = self.y * 4 + self.z
+        self.g = self.x * 2 + self.c
+        self.to_y = {"ctx": self.ctx + 4 * (1 - 2 * self.y), "fsdp": self.z}
+        self.to_x = {"ctx": self.ctx + 2 * (1 - 2 * self.x), "fsdp": self.z}
+        self.to_c = {"ctx": self.ctx + 1 - 2 * self.c, "fsdp": self.z}
+        self.up = {"ctx": self.ctx, "fsdp": self.z + 1}
+        self.dn = {"ctx": self.ctx, "fsdp": self.z - 1}
+        self.sent = []
+
+    def member(self, q):
+        flip, step = q // 4, q % 4
+        z = lax.rem(self.z + step, 4)
+        yy = self.yb if flip else self.y
+        return {"ctx": self.ctx + flip * 4 * (1 - 2 * self.y), "fsdp": z}, yy, z
+
+    def source(self, q):
+        flip, step = q // 4, q % 4
+        return (self.yb if flip else self.y), lax.rem(self.z + 4 - step, 4)
+
+    def barrier(self, members=True, square=True):
+        sem = pltpu.get_barrier_semaphore()
+        peers = [self.member(q)[0] for q in range(1, 8)] if members else []
+        if square:
+            peers += [self.to_x, self.to_c]
+        for peer in peers:
+            pl.semaphore_signal(sem, inc=1, device_id=peer, device_id_type=MESH)
+        pl.semaphore_wait(sem, len(peers))
+
+    def go(self, copy, when=None):
+        if when is None:
+            copy.start()
+        else:
+            pl.when(when)(copy.start)
+        self.sent.append((copy, when))
+
+    def drain(self):
+        for copy, when in self.sent:
+            if when is None:
+                copy.wait_send()
+            else:
+                pl.when(when)(copy.wait_send)
+
+
+def remote(src, dst, send, recv, to):
+    return pltpu.make_async_remote_copy(
+        src_ref=src, dst_ref=dst, send_sem=send, recv_sem=recv, device_id=to, device_id_type=MESH
+    )
+
+
+def arrive(like, recv):
+    pltpu.make_async_copy(like, like, recv).wait()
+
+
+PARTS = ((0, 128), (128, 144))
+
+
+def gather_kernel(xd, ws, es, w2, xdg, wc, eg, w2g, loc, us, ur, ds_, dr, ys, yr, as_, ar, es_, er,
+                  wxs, wxr, wks, wkr, exs, exr, eks, ekr, fxs, fxr, fks, fkr):
+    n = Net()
+    n.barrier()
+
+    def wrow(yy, xx, cc, zz):
+        return wc.at[pl.ds(pl.multiple_of((yy * 16 + xx * 8 + cc * 4 + zz) * 64, 64), 64)]
+
+    def wide(gg):
+        return w2g.at[pl.ds(pl.multiple_of(gg * 256, 256), 256)]
+
+    def thin(gg):
+        return w2g.at[pl.ds(pl.multiple_of(1024 + gg * 64, 64), 64)]
+
+    def shard(zz, p):
+        return xdg.at[n.y * 4 + zz, pl.ds(*PARTS[p])]
+
+    for q in range(1, 8):
+        to, yy, zz = n.member(q)
+        n.go(remote(es.at[yy * 4 + zz], eg.at[n.g * 8 + n.m], es_.at[q], er.at[q], to))
+        n.go(remote(ws.at[yy * 4 + zz], wrow(n.y, n.x, n.c, n.z), as_.at[q], ar.at[q], to))
+    for p in range(2):
+        rows = pl.ds(*PARTS[p])
+        n.go(remote(xd.at[rows], shard(n.z, p), us.at[p, 0], ur.at[p, 0], n.up), n.z < 3)
+        n.go(remote(xd.at[rows], shard(n.z, p), ds_.at[p, 0], dr.at[p, 0], n.dn), n.z > 0)
+        n.go(remote(xd.at[rows], shard(n.z, p), ys.at[p, 0], yr.at[p, 0], n.to_y))
+    halves = ((pl.ds(0, 256), wide), (pl.ds(256, 64), thin))
+    for k, (rows, part) in enumerate(halves):
+        n.go(remote(w2.at[rows], part(n.g), fxs.at[k], fxr.at[k], n.to_x))
+        n.go(remote(w2.at[rows], part(n.g), fks.at[k], fkr.at[k], n.to_c))
+    own = ws.at[n.m]
+    n.go(remote(own, wrow(n.y, n.x, n.c, n.z), wxs.at[0], wxr.at[0], n.to_x))
+    n.go(remote(own, wrow(n.y, n.x, n.c, n.z), wks.at[0], wkr.at[0], n.to_c))
+    local = [
+        pltpu.make_async_copy(xd, xdg.at[n.m], loc.at[0]),
+        pltpu.make_async_copy(own, wrow(n.y, n.x, n.c, n.z), loc.at[1]),
+        pltpu.make_async_copy(es.at[n.m], eg.at[n.g * 8 + n.m], loc.at[2]),
+        pltpu.make_async_copy(w2.at[pl.ds(0, 256)], wide(n.g), loc.at[3]),
+        pltpu.make_async_copy(w2.at[pl.ds(256, 64)], thin(n.g), loc.at[4]),
+    ]
+    for copy in local:
+        copy.start()
+
+    def line(d, p):
+        below, above = n.z >= d, n.z + d <= 3
+
+        @pl.when(below)
+        def _():
+            arrive(shard(n.z - d, p), ur.at[p, d - 1])
+
+        if d < 3:
+            n.go(remote(shard(n.z - d, p), shard(n.z - d, p), us.at[p, d], ur.at[p, d], n.up),
+                 below & (n.z < 3))
+        n.go(remote(shard(n.z - d, p), shard(n.z - d, p), ys.at[p, d], yr.at[p, d], n.to_y), below)
+
+        @pl.when(above)
+        def _():
+            arrive(shard(n.z + d, p), dr.at[p, d - 1])
+
+        if d < 3:
+            n.go(remote(shard(n.z + d, p), shard(n.z + d, p), ds_.at[p, d], dr.at[p, d], n.dn),
+                 above & (n.z > 0))
+        n.go(remote(shard(n.z + d, p), shard(n.z + d, p), ys.at[p, d + 3], yr.at[p, d + 3], n.to_y), above)
+
+    def pieces(qs):
+        for q in qs:
+            yy, zz = n.source(q)
+            block = wrow(yy, n.x, n.c, zz)
+            arrive(block, ar.at[q])
+            n.go(remote(block, block, wxs.at[q], wxr.at[q], n.to_x))
+            n.go(remote(block, block, wks.at[q], wkr.at[q], n.to_c))
+
+    def relay(qs):
+        for q in qs:
+            yy, zz = n.source(q)
+            block = wrow(yy, n.xb, n.c, zz)
+            arrive(block, wxr.at[q])
+            n.go(remote(block, block, wks.at[8 + q], wkr.at[8 + q], n.to_c))
+
+    line(1, 0)
+    pieces((4, 1, 3))
+    line(1, 1)
+    pieces((5, 7, 2, 6))
+    for q in range(1, 8):
+        yy, zz = n.source(q)
+        arrive(eg.at[n.g * 8 + yy * 4 + zz], er.at[q])
+    local[2].wait()
+    mine = eg.at[pl.ds(n.g * 8, 8)]
+    n.go(remote(mine, mine, exs.at[0], exr.at[0], n.to_x))
+    n.go(remote(mine, mine, eks.at[0], ekr.at[0], n.to_c))
+    line(2, 0)
+    line(2, 1)
+    gx = n.xb * 2 + n.c
+    for k, (rows, part) in enumerate(halves):
+        arrive(part(gx), fxr.at[k])
+        n.go(remote(part(gx), part(gx), fks.at[2 + k], fkr.at[2 + k], n.to_c))
+    theirs = eg.at[pl.ds(gx * 8, 8)]
+    relay((0, 4, 1, 3))
+    line(3, 0)
+    relay((5, 7, 2, 6))
+    arrive(theirs, exr.at[0])
+    n.go(remote(theirs, theirs, eks.at[1], ekr.at[1], n.to_c))
+    line(3, 1)
+    for q in range(8):
+        yy, zz = n.source(q)
+        arrive(wrow(yy, n.x, n.cb, zz), wkr.at[q])
+        arrive(wrow(yy, n.xb, n.cb, zz), wkr.at[8 + q])
+    for k in range(2):
+        arrive(eg.at[pl.ds((2 * (n.xb if k else n.x) + n.cb) * 8, 8)], ekr.at[k])
+        for j, (rows, part) in enumerate(halves):
+            arrive(part(2 * (n.xb if k else n.x) + n.cb), fkr.at[2 * k + j])
+    for p in range(2):
+        rows = pl.ds(*PARTS[p])
+        arrive(xdg.at[n.yb * 4 + n.z, rows], yr.at[p, 0])
+        for d in range(1, 4):
+            @pl.when(n.z >= d)
+            def _():
+                arrive(xdg.at[n.yb * 4 + n.z - d, rows], yr.at[p, d])
+
+            @pl.when(n.z + d <= 3)
+            def _():
+                arrive(xdg.at[n.yb * 4 + n.z + d, rows], yr.at[p, d + 3])
+    for k in (0, 1, 3, 4):
+        local[k].wait()
+    n.drain()
+
+
+def gather_all(xd, ws, es, w2):
+    sd = jax.ShapeDtypeStruct
+    return pl.pallas_call(
+        gather_kernel,
+        name="gather_all",
+        out_shape=(sd((8, 272, 2048), BF), sd((2048, 1792), BF), sd((32, 8, 1792), BF), sd((1280, 2048), BF)),
+        in_specs=[VM] * 4,
+        out_specs=(HBM,) * 4,
+        scratch_shapes=[DMA((5,)), DMA((2, 3)), DMA((2, 3)), DMA((2, 3)), DMA((2, 3)), DMA((2, 7)), DMA((2, 7)),
+                        DMA((8,)), DMA((8,)), DMA((8,)), DMA((8,)), DMA((8,)), DMA((8,)), DMA((16,)), DMA((16,)),
+                        DMA((1,)), DMA((1,)), DMA((2,)), DMA((2,)), DMA((2,)), DMA((2,)), DMA((4,)), DMA((4,))],
+        compiler_params=pltpu.CompilerParams(collective_id=1, has_side_effects=True, vmem_limit_bytes=VLIM),
+    )(xd, ws, es, w2)
+
+
+def exchange_kernel(src, dst, loc, ss, rs):
+    n = Net()
+    n_peer = {"ctx": n.ctx + 2 * (1 - 2 * n.x) + 1 - 2 * n.c, "fsdp": n.z}
+    sem = pltpu.get_barrier_semaphore()
+    for peer in (n.to_x, n.to_c, n_peer):
+        pl.semaphore_signal(sem, inc=1, device_id=peer, device_id_type=MESH)
+    pl.semaphore_wait(sem, 3)
+    copies = []
+    for k, (to, gg) in enumerate(((n_peer, 2 * n.xb + n.cb), (n.to_x, 2 * n.xb + n.c), (n.to_c, 2 * n.x + n.cb))):
+        copies.append(remote(src.at[gg], dst.at[n.g], ss.at[k], rs.at[k], to))
+    for copy in copies:
+        copy.start()
+    own = pltpu.make_async_copy(src.at[n.g], dst.at[n.g], loc)
+    own.start()
+    own.wait()
+    for copy in copies:
+        copy.wait()
+
+
+def exchange(a, cid):
+    return pl.pallas_call(
+        exchange_kernel,
+        name="exchange",
+        out_shape=jax.ShapeDtypeStruct(a.shape, a.dtype),
+        in_specs=[VM],
+        out_specs=VM,
+        scratch_shapes=[DMA, DMA((3,)), DMA((3,))],
+        compiler_params=pltpu.CompilerParams(collective_id=cid, has_side_effects=True, vmem_limit_bytes=VLIM),
+    )(a)
+
+
+def lanes_of(shape):
+    return lax.broadcasted_iota(jnp.int32, shape, len(shape) - 1)
+
+
+def partner(t):
+    low = lax.rem(lanes_of(t.shape), 64) < 16
+    return jnp.where(low, pltpu.roll(t, 112, 1), pltpu.roll(t, 16, 1))
+
+
+def dot_nt(a, b):
+    return lax.dot_general(a, b, (((1,), (1,)), ((), ())), preferred_element_type=F32)
+
+
+def dot_tn(a, b):
+    return lax.dot_general(a, b, (((0,), (0,)), ((), ())), preferred_element_type=F32)
+
+
+def project_kernel(xd, wc, w2, gain, bias, wbias, cos, sin, normed_o, qkvd_o, act_o, dup_o, dsum_o):
+    xf = xd[0, 0:128, :].astype(F32)
+    mean = jnp.mean(xf, axis=-1, keepdims=True)
+    cen = xf - mean
+    rstd = lax.rsqrt(jnp.mean(cen * cen, axis=-1, keepdims=True) + EPS)
+    normed = (cen * rstd * gain[...] + bias[...]).astype(BF)
+    normed_o[...] = normed
+    dy = xd[0, 128:256, :]
+    dd = dot_nt(dy, w2[1024:1280, :])
+    half = lanes_of((128, 128)) < 64
+    cosv, sinv = cos[0], sin[0]
+    proj = jnp.dot(normed, wc[:, 0:768], preferred_element_type=F32) + wbias[:, 0:768]
+    for g in range(4):
+        t = proj[:, 128 * g : 128 * g + 128]
+        qkvd_o[g, 0, :, 0:128] = (t * cosv + partner(t) * sinv).astype(BF)
+        v = proj[:, 512 + 128 * (g // 2) : 640 + 128 * (g // 2)]
+        d = dd[:, 128 * (g // 2) : 128 * (g // 2) + 128]
+        if g % 2 == 0:
+            vd = jnp.where(half, v, pltpu.roll(d, 64, 1))
+        else:
+            vd = jnp.where(half, pltpu.roll(v, 64, 1), d)
+        qkvd_o[g, 0, :, 128:256] = vd.astype(BF)
+    for k in range(4):
+        cols = slice(256 * k, 256 * k + 256)
+        up = jnp.dot(normed, wc[:, 768 + 256 * k : 1024 + 256 * k], preferred_element_type=F32)
+        act, slope = gelu_pair(up + wbias[:, 768 + 256 * k : 1024 + 256 * k])
+        act_o[:, cols] = act.astype(BF)
+        dup = dot_nt(dy, w2[256 * k : 256 * k + 256, :]) * slope
+        dup_o[:, cols] = dup.astype(BF)
+        dsum = jnp.broadcast_to(jnp.sum(dup, axis=0, keepdims=True), (8, 256))
+
+        @pl.when(pl.program_id(0) == 0)
+        def _():
+            dsum_o[:, cols] = dsum
+
+        @pl.when(pl.program_id(0) > 0)
+        def _():
+            dsum_o[:, cols] += dsum
+
+
+def project(xdg, wc, w2g, gain, bias, wbias, cos, sin):
+    sd = jax.ShapeDtypeStruct
+    one = pl.Buffered(1)
+
+    def whole(shape):
+        return pl.BlockSpec(shape, lambda i: (0,) * len(shape), pipeline_mode=one)
+
+    return pl.pallas_call(
+        project_kernel,
+        name="project",
+        grid=(8,),
+        out_shape=(sd((1024, 2048), BF), sd((4, 8, 128, 256), BF), sd((1024, 1024), BF), sd((1024, 1024), BF),
+                   sd((8, 1024), F32)),
+        in_specs=[
+            pl.BlockSpec((1, 272, 2048), lambda i: (i, 0, 0)),
+            whole((2048, 1792)),
+            whole((1280, 2048)),
+            whole((1, 2048)),
+            whole((1, 2048)),
+            whole((1, 1792)),
+            pl.BlockSpec((1, 128, 128), lambda i: (i // 4, 0, 0)),
+            pl.BlockSpec((1, 128, 128), lambda i: (i // 4, 0, 0)),
+        ],
+        out_specs=(
+            pl.BlockSpec((128, 2048), lambda i: (i, 0)),
+            pl.BlockSpec((4, 1, 128, 256), lambda i: (0, i, 0, 0)),
+            pl.BlockSpec((128, 1024), lambda i: (i, 0)),
+            pl.BlockSpec((128, 1024), lambda i: (i, 0)),
+            pl.BlockSpec((8, 1024), lambda i: (0, 0)),
+        ),
+        compiler_params=pltpu.CompilerParams(vmem_limit_bytes=VLIM),
+    )(xdg, wc, w2g, gain, bias, wbias, cos, sin)
+
+
+def attention_kernel(slot_of, a, doc_row, doc_col, cos, sin, out, sums, seq, att, dq, dk, dv):
+    def where_is(p):
+        r = slot_of[p]
+        ctx = lax.div(r, 2)
+        return lax.rem(ctx, 4), lax.div(ctx, 4), pl.ds(pl.multiple_of(lax.rem(r, 2) * 64, 64), 64)
+
+    for p in range(16):
+        g, yy, rows = where_is(p)
+        seq[64 * p : 64 * p + 64, :] = a[g, yy, 0, rows, :]
+    dk[...] = jnp.zeros_like(dk)
+    dv[...] = jnp.zeros_like(dv)
+    scale = 0.125
+    low = lanes_of((256, 128)) < 64
+    for i in range(4):
+        k0 = max(0, i - 2) * 256
+        kn = 256 * (i + 1) - k0
+        rq, rk = slice(256 * i, 256 * i + 256), slice(k0, k0 + kn)
+        qk, vd = seq[rq, 0:128], seq[rq, 128:256]
+        kk, vv = seq[rk, 0:128], seq[rk, 128:256]
+        zero = jnp.zeros((256, 128), F32)
+        qs = jnp.where(low, zero, pltpu.roll(qk.astype(F32), 64, 1)).astype(BF)
+        dsf = jnp.where(low, pltpu.roll(vd.astype(F32), 64, 1), zero)
+        s = dot_nt(qs, kk) * scale
+        qpos = 256 * i + lax.broadcasted_iota(jnp.int32, (256, kn), 0)
+        kpos = k0 + lax.broadcasted_iota(jnp.int32, (256, kn), 1)
+        mask = (kpos <= qpos) & (doc_row[0, :, rk] == doc_col[0, rq, :])
+        s = jnp.where(mask, s, NEG)
+        top = jnp.max(s, axis=-1, keepdims=True)
+        e = jnp.where(mask, jnp.exp(s - top), 0.0)
+        inv = 1.0 / jnp.sum(e, axis=-1, keepdims=True)
+        o = jnp.dot(e.astype(BF), vv, preferred_element_type=F32) * inv
+        ob = o.astype(BF)
+        att[rq, :] = ob.astype(F32)
+        delta = jnp.sum(dsf * ob.astype(F32), axis=-1, keepdims=True)
+        pr = e * inv
+        dv[rk, :] += dot_tn(pr.astype(BF), vd)
+        dp = dot_nt(dsf.astype(BF), vv)
+        ds = (pr * (dp - delta) * scale).astype(BF)
+        dq[rq, :] = jnp.dot(ds, kk, preferred_element_type=F32)
+        dk[rk, :] += dot_tn(ds, qk)
+    tot = jnp.zeros((8, 256), F32)
+    half = lanes_of((64, 128)) < 64
+    s1 = jnp.zeros((1, 128), F32)
+    s2 = jnp.zeros((1, 128), F32)
+    for p in range(16):
+        rows = slice(64 * p, 64 * p + 64)
+        g, yy, place_rows = where_is(p)
+        t = jnp.where(half, pltpu.roll(dq[rows, :], 64, 1), pltpu.roll(dk[rows, :], 64, 1))
+        t = t * cos[rows, :] - partner(t) * sin[rows, :]
+        u = jnp.where(half, pltpu.roll(dv[rows, :], 64, 1), pltpu.roll(att[rows, :], 64, 1))
+        s1 += jnp.sum(t, axis=0, keepdims=True)
+        s2 += jnp.sum(u, axis=0, keepdims=True)
+        out[g, yy, 0, place_rows, 0:128] = t.astype(BF)
+        out[g, yy, 0, place_rows, 128:256] = u.astype(BF)
+    sums[0, :, 0:128] = jnp.broadcast_to(s1, (8, 128))
+    sums[0, :, 128:256] = jnp.broadcast_to(s2, (8, 128))
+
+
+def attention(slot_of, a, docs, cos, sin):
+    sd = jax.ShapeDtypeStruct
+    blk = pl.BlockSpec((4, 2, 1, 128, 256), lambda s, t: (0, 0, s, 0, 0))
+    return pl.pallas_call(
+        attention_kernel,
+        name="attention",
+        grid_spec=pltpu.PrefetchScalarGridSpec(
+            num_scalar_prefetch=1,
+            grid=(4,),
+            in_specs=[
+                blk,
+                pl.BlockSpec((1, 1, 1024), lambda s, t: (s, 0, 0)),
+                pl.BlockSpec((1, 1024, 1), lambda s, t: (s, 0, 0)),
+                pl.BlockSpec((1024, 128), lambda s, t: (0, 0)),
+                pl.BlockSpec((1024, 128), lambda s, t: (0, 0)),
+            ],
+            out_specs=(blk, pl.BlockSpec((1, 8, 256), lambda s, t: (s, 0, 0))),
+            scratch_shapes=[pltpu.VMEM((1024, 256), BF)] + [pltpu.VMEM((1024, 128), F32)] * 4,
+        ),
+        out_shape=(sd((4, 2, 4, 128, 256), BF), sd((4, 8, 256), F32)),
+        compiler_params=pltpu.CompilerParams(vmem_limit_bytes=VLIM),
+    )(slot_of, a, docs[:, None, :], docs[:, :, None], cos, sin)
+
+
+def add_rows(dst, srcs, rows, out=None, step=16):
+    out = dst if out is None else out
+
+    def body(i, carry):
+        sl = pl.ds(pl.multiple_of(i * step, step), step)
+        v = dst[sl, :].astype(F32)
+        for s in srcs:
+            v = v + s[sl, :].astype(F32)
+        out[sl, :] = v.astype(out.dtype)
+        return carry
+
+    lax.fori_loop(0, rows // step, body, 0)
+
+
+def reduce_kernel(part, dw1, dw2, e1, yo, o1, o2, eo, own, yr, ub, db, w1, r1, r2, w2, s1, s2, ev, t1, t2,
+                  ol, wl, vl, yss, yrs, uss, urs, dss, drs, k1s, k1r, x1s, x1r, a1s, a1r,
+                  k2s, k2r, x2s, x2r, eks, ekr, exs, exr, eas, ear, fl):
+    n = Net()
+    n.barrier()
+    order = (3, 0, 2, 1)
+
+    def block(yy, xx, cc):
+        return dw1.at[pl.ds(pl.multiple_of((yy * 16 + xx * 8 + cc * 4) * 64, 256), 256)]
+
+    def wide(gg):
+        return dw2.at[pl.ds(pl.multiple_of(gg * 256, 256), 256)]
+
+    def thin(gg):
+        return dw2.at[pl.ds(pl.multiple_of(1024 + gg * 64, 64), 64)]
+
+    load_own = {}
+    for t in range(2):
+        for k in order:
+            n.go(remote(part.at[n.yb * 4 + k, t], yr.at[k, t], yss.at[t, k], yrs.at[t, k], n.to_y))
+    for xx in range(2):
+        gg = 2 * xx + n.cb
+        n.go(remote(e1.at[pl.ds(gg * 8, 8)], t1.at[xx], eks.at[xx], ekr.at[xx], n.to_c))
+        n.go(remote(wide(gg), s1.at[xx, pl.ds(0, 256)], k2s.at[xx, 0], k2r.at[xx, 0], n.to_c))
+        n.go(remote(thin(gg), s1.at[xx, pl.ds(256, 64)], k2s.at[xx, 1], k2r.at[xx, 1], n.to_c))
+        for yy in range(2):
+            n.go(remote(block(yy, xx, n.cb), r1.at[yy * 2 + xx], k1s.at[yy * 2 + xx], k1r.at[yy * 2 + xx], n.to_c))
+    loads = []
+    for xx in range(2):
+        gg = 2 * xx + n.c
+        loads.append(pltpu.make_async_copy(e1.at[pl.ds(gg * 8, 8)], ev.at[xx], vl.at[xx, 0]))
+        loads.append(pltpu.make_async_copy(wide(gg), w2.at[xx, pl.ds(0, 256)], vl.at[xx, 1]))
+        loads.append(pltpu.make_async_copy(thin(gg), w2.at[xx, pl.ds(256, 64)], vl.at[xx, 2]))
+        for yy in range(2):
+            loads.append(pltpu.make_async_copy(block(yy, xx, n.c), w1.at[yy * 2 + xx], wl.at[yy * 2 + xx]))
+    for t in range(2):
+        for k in order:
+            load_own[t, k] = pltpu.make_async_copy(part.at[n.y * 4 + k, t], own.at[k, t], ol.at[t, k])
+    for copy in loads + list(load_own.values()):
+        copy.start()
+    for copy in loads:
+        copy.wait()
+
+    for xx in range(2):
+        arrive(t1.at[xx], ekr.at[xx])
+        ev[xx] = ev[xx] + t1[xx]
+        arrive(s1.at[xx, pl.ds(0, 256)], k2r.at[xx, 0])
+        arrive(s1.at[xx, pl.ds(256, 64)], k2r.at[xx, 1])
+        add_rows(w2.at[xx], [s1.at[xx]], 320)
+        for yy in range(2):
+            arrive(r1.at[yy * 2 + xx], k1r.at[yy * 2 + xx])
+            add_rows(w1.at[yy * 2 + xx], [r1.at[yy * 2 + xx]], 256)
+    n.go(remote(ev.at[n.xb], t2, exs.at[0], exr.at[0], n.to_x))
+    for yy in range(2):
+        n.go(remote(w1.at[yy * 2 + n.xb], r2.at[yy], x1s.at[yy], x1r.at[yy], n.to_x))
+    n.go(remote(w2.at[n.xb], s2, x2s.at[0], x2r.at[0], n.to_x))
+
+    def forward(t, k):
+        def send_up():
+            return remote(own.at[k, t], ub.at[k, t], uss.at[t, k], urs.at[t, k], n.up)
+
+        def send_down():
+            return remote(own.at[k, t], db.at[k, t], dss.at[t, k], drs.at[t, k], n.dn)
+
+        @pl.when(n.z != k)
+        def _():
+            load_own[t, k].wait()
+            arrive(yr.at[k, t], yrs.at[t, k])
+        if k > 0:
+            @pl.when(n.z == 0)
+            def _():
+                add_rows(own.at[k, t], [yr.at[k, t]], 128)
+
+            if k > 1:
+                @pl.when((n.z > 0) & (n.z < k))
+                def _():
+                    arrive(ub.at[k, t], urs.at[t, k])
+                    add_rows(own.at[k, t], [yr.at[k, t], ub.at[k, t]], 128)
+
+            n.go(send_up(), n.z < k)
+        if k < 3:
+            @pl.when(n.z == 3)
+            def _():
+                add_rows(own.at[k, t], [yr.at[k, t]], 128)
+
+            if k < 2:
+                @pl.when((n.z < 3) & (n.z > k))
+                def _():
+                    arrive(db.at[k, t], drs.at[t, k])
+                    add_rows(own.at[k, t], [yr.at[k, t], db.at[k, t]], 128)
+
+            n.go(send_down(), n.z > k)
+
+    def finish(t, k):
+        @pl.when(n.z == k)
+        def _():
+            load_own[t, k].wait()
+            arrive(yr.at[k, t], yrs.at[t, k])
+            more = [yr.at[k, t]]
+            if k > 0:
+                arrive(ub.at[k, t], urs.at[t, k])
+                more.append(ub.at[k, t])
+            if k < 3:
+                arrive(db.at[k, t], drs.at[t, k])
+                more.append(db.at[k, t])
+            add_rows(own.at[k, t], more, 128, yo.at[t])
+
+    for k in order:
+        forward(0, k)
+    arrive(t2, exr.at[0])
+    ev[n.x] = ev[n.x] + t2[...]
+    for q in range(1, 8):
+        to, yy, zz = n.member(q)
+        n.go(remote(ev.at[n.x, yy * 4 + zz], eo.at[n.m], eas.at[q], ear.at[q], to))
+    eo[n.m] = ev[n.x, n.m]
+    for yy in range(2):
+        arrive(r2.at[yy], x1r.at[yy])
+        add_rows(w1.at[yy * 2 + n.x], [r2.at[yy]], 256)
+    for q in (4, 1, 3, 5, 7, 2, 6):
+        to, yy, zz = n.member(q)
+        n.go(remote(w1.at[yy * 2 + n.x, pl.ds(pl.multiple_of(zz * 64, 64), 64)], o1.at[n.m], a1s.at[q], a1r.at[q], to))
+    mine = pltpu.make_async_copy(w1.at[n.y * 2 + n.x, pl.ds(pl.multiple_of(n.z * 64, 64), 64)], o1.at[n.m], fl.at[0])
+    mine.start()
+    for k in order:
+        forward(1, k)
+    arrive(s2, x2r.at[0])
+    add_rows(w2.at[n.x], [s2], 320, o2)
+    for t in range(2):
+        for k in range(4):
+            finish(t, k)
+    for q in range(1, 8):
+        yy, zz = n.source(q)
+        arrive(eo.at[yy * 4 + zz], ear.at[q])
+        arrive(o1.at[yy * 4 + zz], a1r.at[q])
+    mine.wait()
+    n.drain()
+
+
+def reduce_all(part, dw1, dw2, e1):
+    sd = jax.ShapeDtypeStruct
+    V = pltpu.VMEM
+    return pl.pallas_call(
+        reduce_kernel,
+        name="reduce_all",
+        out_shape=(sd((2, 128, 2048), F32), sd((8, 64, 1792), BF), sd((320, 2048), F32), sd((8, 16, 128), F32)),
+        in_specs=[HBM, HBM, HBM, VM],
+        out_specs=(VM, VM, VM, VM),
+        scratch_shapes=[
+            V((4, 2, 128, 2048), BF), V((4, 2, 128, 2048), BF), V((4, 2, 128, 2048), BF), V((4, 2, 128, 2048), BF),
+            V((4, 256, 1792), BF), V((4, 256, 1792), BF), V((2, 256, 1792), BF),
+            V((2, 320, 2048), BF), V((2, 320, 2048), BF), V((320, 2048), BF),
+            V((2, 8, 16, 128), F32), V((2, 8, 16, 128), F32), V((8, 16, 128), F32),
+            DMA((2, 4)), DMA((4,)), DMA((2, 3)),
+            DMA((2, 4)), DMA((2, 4)), DMA((2, 4)), DMA((2, 4)), DMA((2, 4)), DMA((2, 4)),
+            DMA((4,)), DMA((4,)), DMA((2,)), DMA((2,)), DMA((8,)), DMA((8,)),
+            DMA((2, 2)), DMA((2, 2)), DMA((1,)), DMA((1,)),
+            DMA((2,)), DMA((2,)), DMA((1,)), DMA((1,)), DMA((8,)), DMA((8,)), DMA((1,)),
+        ],
+        compiler_params=pltpu.CompilerParams(collective_id=3, has_side_effects=True, vmem_limit_bytes=VLIM),
+    )(part, dw1, dw2, e1)
+
+
+def member_columns(qkv, ff):
+    rows = qkv.shape[0]
+    parts = qkv.reshape(rows, 3, 2, 4, 4, 64)
+    qk = parts[:, :2].transpose(2, 4, 0, 3, 1, 5).reshape(8, rows, 512)
+    v = parts[:, 2].transpose(1, 3, 0, 2, 4).reshape(8, rows, 256)
+    f = ff.reshape(rows, 2, 4, 4, 256).transpose(1, 3, 0, 2, 4).reshape(8, rows, 1024)
+    return jnp.concatenate([qk, v, f], axis=2)
+
+
+def stored_columns(a):
+    rows = a.shape[1]
+    qk = a[:, :, :512].reshape(2, 4, rows, 4, 2, 64).transpose(2, 4, 0, 3, 1, 5).reshape(rows, 2, 2048)
+    v = a[:, :, 512:768].reshape(2, 4, rows, 4, 64).transpose(2, 0, 3, 1, 4).reshape(rows, 1, 2048)
+    f = a[:, :, 768:1792].reshape(2, 4, rows, 4, 256).transpose(2, 0, 3, 1, 4).reshape(rows, 8192)
+    return jnp.concatenate([qk, v], axis=1).reshape(rows, 6144), f
+
+
+def rotary_lanes(pos):
+    half = ROT // 2
+    freqs = jnp.exp(-(2.0 * jnp.arange(half, dtype=F32) / ROT) * math.log(10000.0))
+    angles = pos.astype(F32)[..., None] * freqs
+    c, s = jnp.cos(angles), jnp.sin(angles)
+    one = jnp.ones(pos.shape + (32,), F32)
+    cos = jnp.concatenate([c, c, one] * 2, axis=-1)
+    sin = jnp.concatenate([-s, s, 0.0 * one] * 2, axis=-1)
+    return cos, sin
+
+
+def fast_device(
+    block_input, output_grad, segment, slots, ln_gain, ln_bias, qkv_w, qkv_b, dense_w, dense_b, fc1_w, fc1_b, fc2_w, fc2_b
+):
+    ctx, y, x, c, z = place()
+    g, m = x * 2 + c, y * 4 + z
+    index = ctx * 4 + z
+    xb, dyb = block_input[0], output_grad[0]
+
+    docs = jnp.zeros((16, 2048), BF).at[0, :1024].set(segment[0].astype(BF))
+    xd = jnp.concatenate([xb, dyb, docs], axis=0)
+    ws = member_columns(qkv_w, fc1_w)
+
+    def spread(piece, total):
+        return lax.dynamic_update_slice(jnp.zeros((total,), BF), piece, (index * piece.shape[0],))
+
+    wb = member_columns(spread(qkv_b, 6144)[None], spread(fc1_b, 8192)[None])
+    small = jnp.stack([spread(v, 2048) for v in (ln_gain, ln_bias, dense_b, fc2_b)])
+    rest = jnp.zeros((1792,), BF).at[:1024].set(small[:, 1792:].reshape(1024))
+    es = jnp.concatenate([jnp.concatenate([small[:, :1792], rest[None], jnp.zeros((2, 1792), BF)])[None]] * 8)
+    es = jnp.concatenate([wb, es], axis=1)
+    w2 = jnp.concatenate([fc2_w, dense_w], axis=0)
+    xdg, wc, eg, w2g = gather_all(xd, ws, es, w2)
+
+    ext = jnp.sum(eg.astype(F32), axis=0)
+    wbias = ext[0:1]
+    vecs = jnp.concatenate([ext[1:5], ext[5, :1024].reshape(4, 256)], axis=1)
+    gain, lnb, ob = vecs[0:1], vecs[1:2], vecs[2:3] + vecs[3:4]
+    pos_of_row = slots[:, None] * 64 + jnp.arange(64, dtype=jnp.int32)[None]
+    rows2 = lax.dynamic_slice_in_dim(pos_of_row.reshape(2, 4, 128), g, 1, 1).reshape(2, 128)
+    cos, sin = rotary_lanes(rows2)
+    normed, qkvd, act, dup, dsum = project(xdg, wc, w2g, gain, lnb, wbias, cos, sin)
+
+    heads_in = exchange(qkvd.reshape(4, 1024, 256), 2)
+    slot_of = jnp.sum(jnp.where(slots[None, :] == jnp.arange(16, dtype=jnp.int32)[:, None], jnp.arange(16, dtype=jnp.int32)[None, :], 0), axis=1)
+    cosp, sinp = rotary_lanes(jnp.arange(1024, dtype=jnp.int32))
+    docs4 = xdg[0:4, 256, 0:1024].astype(F32)
+    att, sums = attention(slot_of, heads_in.reshape(4, 2, 4, 128, 256), docs4, cosp, sinp)
+    back = exchange(att.reshape(4, 1024, 256), 4)
+
+    dqk = back[:, :, 0:128].transpose(1, 0, 2).reshape(1024, 512)
+    dvv = back[:, :, 128:192].transpose(1, 0, 2).reshape(1024, 256)
+    attn = back[:, :, 192:256].transpose(1, 0, 2).reshape(1024, 256)
+    dpr = jnp.concatenate([dqk, dvv, dup], axis=1)
+    up2 = jnp.concatenate([act, attn], axis=1)
+    dy_all = xdg[:, 128:256].reshape(1024, 2048)
+    ypart = jnp.dot(up2, w2g, preferred_element_type=F32)
+    dn = contract_cols(dpr, wc)
+    xf = xdg[:, 0:128].reshape(1024, 2048).astype(F32)
+    cen = xf - jnp.mean(xf, axis=-1, keepdims=True)
+    xhat = cen * lax.rsqrt(jnp.mean(cen * cen, axis=-1, keepdims=True) + EPS)
+    gpart = jnp.sum(dn * xhat, axis=0)
+    bpart = jnp.sum(dn, axis=0)
+    dw1 = contract_rows(normed, dpr).astype(BF)
+    dw2 = contract_rows(up2, dy_all).astype(BF)
+    part = jnp.stack([ypart.astype(BF).reshape(8, 128, 2048), dn.astype(BF).reshape(8, 128, 2048)], axis=1)
+
+    hs = jnp.sum(sums[:, 0, :], axis=0)
+    colq = lax.dynamic_update_slice(jnp.zeros((512,), F32), hs[:128], (g * 128,))
+    colv = lax.dynamic_update_slice(jnp.zeros((256,), F32), hs[128:192], (g * 64,))
+    cols = jnp.concatenate([colq, colv, dsum[0]])
+
+    def rows_of(v):
+        return v.reshape(2, 4, 4, 64).transpose(1, 0, 2, 3).reshape(32, 64)
+
+    dsum_y = jnp.sum(dy_all.astype(F32), axis=0)
+    e1 = jnp.concatenate(
+        [jnp.broadcast_to(cols, (32, 1792)), rows_of(gpart), rows_of(bpart), rows_of(dsum_y), jnp.zeros((32, 64), F32)], axis=1
+    ).reshape(32, 16, 128)
+    yo, o1, o2, eo = reduce_all(part, dw1, dw2, e1)
+
+    xf = xb.astype(F32)
+    cen = xf - jnp.mean(xf, axis=-1, keepdims=True)
+    rstd = lax.rsqrt(jnp.mean(cen * cen, axis=-1, keepdims=True) + EPS)
+    xhat = cen * rstd
+    out = (xf + yo[0] + ob).astype(BF)
+    gr = yo[1] * gain
+    dx = dyb.astype(F32) + rstd * (
+        gr - jnp.mean(gr, axis=-1, keepdims=True) - xhat * jnp.mean(gr * xhat, axis=-1, keepdims=True)
+    )
+    g_qkv_w, g_fc1_w = stored_columns(o1.astype(F32))
+    eo = eo.reshape(8, 2048)
+    sq, sf = stored_columns(eo[:, None, :1792])
+    g_qkv_b = lax.dynamic_slice_in_dim(sq[0], index * 192, 192, 0)
+    g_fc1_b = lax.dynamic_slice_in_dim(sf[0], index * 256, 256, 0)
+    g_gain = jnp.sum(eo[:, 1792:1856], axis=0)
+    g_lnb = jnp.sum(eo[:, 1856:1920], axis=0)
+    g_db = eo[0, 1920:1984]
+    return (out[None], dx[None], g_gain, g_lnb, g_qkv_w, g_qkv_b, o2[256:], g_db, g_fc1_w, g_fc1_b, o2[:256], g_db)
+
+
 def solution(mesh):
     in_specs = (
         P("fsdp", "ctx", None),
@@ -351,6 +1067,7 @@
         P(("ctx", "fsdp"), None),
         P(("ctx", "fsdp")),
     )
+    small = mesh.shape["ctx"] == 8 and mesh.shape["fsdp"] == 4
     return jax.shard_map(
-        per_device, mesh=mesh, in_specs=in_specs, out_specs=out_specs, check_vma=False
-    )
+        fast_device if small else per_device, mesh=mesh, in_specs=in_specs, out_specs=out_specs, check_vma=False
+    )

time: 1750 us -> 550 us (0.31)
  waiting for transfers between devices: 1170 us -> 0 us
  Pallas kernels: 0 us -> 399 us
  matrix products: 220 us -> 38.2 us
  blocking collectives: 124 us -> 0 us
  other arithmetic: 86.3 us -> 30.7 us
  local copies, waits for them, and re-layouts: 95.9 us -> 71.2 us
  starting transfers between devices: 24.6 us -> 0 us
    all_gather x12 -> x0, waiting for transfers between devices: 608 us -> none  [the longest x1 142 us: per_device(): lax.all_gather(dup_b, 'fsdp', axis=0, tiled=True)]
    pallas_call x0 -> x6, Pallas kernels: none -> 399 us  [the longest x1 150 us: reduce_all(): pl.pallas_call(reduce_kernel, name='reduce_all', out_shape=(sd((2, 128, 2...]
    ppermute x32 -> x0, waiting for transfers between devices: 267 us -> none  [shifted(): return lax.ppermute(block, axis, route)]
    reduce_scatter x4 -> x0, waiting for transfers between devices: 204 us -> none  [the longest x1 72.5 us: per_device(): lax.psum_scatter(contract_rows(own_normed, group_dup).astype(jnp.bfloat16...]
    dot_general x46 -> x1, matrix products: 130 us -> 7.11 us  [fast_device(): ypart = jnp.dot(up2, w2g, preferred_element_type=F32)]
    unnamed x18 -> x0, waiting for transfers between devices: 94.9 us -> none
    all_gather x1 -> x0, blocking collectives: 66.7 us -> none  [per_device(): lax.all_gather(fc1_b, ('ctx', 'fsdp'), axis=0, tiled=True)]
    convert_element_type x45 -> x5, other arithmetic: 61.7 us -> 2.35 us  [the longest x2 2.33 us: fast_device(): docs4 = xdg[0:4, 256, 0:1024].astype(F32)]
  transfers between devices with their start and end apart: 49 -> 0, of which waited for: 44 -> 0; matrix products, arithmetic and copies ran while one was open for 23% -> 0% of each run, Pallas kernels for 0% -> 0%
where the time goes in v1:
time: 550 us; the launch traced here: 541 us
  Pallas kernels  399 us (73%)
  local copies, waits for them, and re-layouts  71.2 us (13%)
  matrix products  38.2 us (7%)
  other arithmetic  30.7 us (6%)
    pallas_call x1, Pallas kernels, reduce_all(): pl.pallas_call(reduce_kernel, name='reduce_all', out_shape=(sd((2, 128, 2...  150 us
    pallas_call x1, Pallas kernels, gather_all(): pl.pallas_call(gather_kernel, name='gather_all', out_shape=(sd((8, 272, 2...  126 us
    pallas_call x2, Pallas kernels, exchange(): pl.pallas_call(exchange_kernel, name='exchange', out_shape=jax.ShapeDtype...  56.9 us
    pallas_call x1, Pallas kernels, project(): pl.pallas_call(project_kernel, name='project', grid=(8,), out_shape=(sd((...  43.7 us
    pallas_call x1, Pallas kernels, attention(): pl.pallas_call(attention_kernel, name='attention', grid_spec=pltpu.Prefet...  21.9 us
    dot_general x2, matrix products, contract_rows(): lax.dot_general(left, right, (((0,), (0,)), ((), ())), preferred_element_...  17.9 us
    dot_general x1, matrix products, contract_cols(): lax.dot_general(left, right, (((1,), (1,)), ((), ())), preferred_element_...  13.2 us

profile of v1, /device:TPU:8, one launch (start us, length us, event | category | flops | bytes accessed | tf_op | source)
XLA Modules:
  0.0 540.9 jit_solution(10048715905736470250)
XLA Ops:
  7.4 2.5 reshape.338
  18.1 2.1 pad_maximum_fusion.8.w2
  21.3 126.3 %gather_all.1 = (bf16[8,272,2048]{2,1,0:T(8,128)(2,1)}, bf16[2048,1792]{1,0:T(8,128)(2,1)}, bf16[32,8,1792]{2,1,0:T(8,128)(2,1)}, bf16[1280,2048]{1,0:T(8,128)(2,1)}) custom-call(bf16[272,2048]{1,0:T(8,128)(2,1)} %fusion.7.xd, bf16[8,64,1792]{2,1,0:T(8,128)(2,1)} %pad_maximum_fusion.3.ws, bf16[8,8,1792]{2,1,0:T(8,128)(2,1)} %pad_maximum_fusion.9.es, ...), custom_call_target="tpu_custom_call" | custom-call | tf_op jit(solution)/shard_map/gather_all/pallas_call | solution.py:528
  153.0 43.7 %project.1 = (bf16[1024,2048]{1,0:T(8,128)(2,1)}, bf16[4,8,128,256]{3,2,1,0:T(8,128)(2,1)}, bf16[1024,1024]{1,0:T(8,128)(2,1)}, bf16[1024,1024]{1,0:T(8,128)(2,1)}, f32[8,1024]{1,0:T(8,128)}) custom-call(bf16[8,272,2048]{2,1,0:T(8,128)(2,1)} %get-tuple-element.51.xd, bf16[2048,1792]{1,0:T(8,128)(2,1)} %get-tuple-element.52.wc, ...), custom_call_target="tpu_custom_call" | custom-call | tf_op jit(solution)/shard_map/project/pallas_call | solution.py:636
  196.6 28.4 %exchange.2 = bf16[4,1024,256]{2,1,0:T(8,128)(2,1)} custom-call(bf16[4,1024,256]{2,1,0:T(8,128)(2,1)} %bitcast.140), custom_call_target="tpu_custom_call" | custom-call | tf_op jit(solution)/shard_map/exchange/pallas_call | solution.py:561
  235.5 21.9 %attention.1 = (bf16[4,2,4,128,256]{4,3,2,1,0:T(8,128)(2,1)}, f32[4,8,256]{2,1,0:T(8,128)}) custom-call(s32[16]{0:T(128)} %select_reduce_fusion.slot_of, bf16[4,2,4,128,256]{4,3,2,1,0:T(8,128)(2,1)} %bitcast.125, f32[4,1,1024]{2,1,0:T(1,128)} %slice_convert_fusion.doc_row, f32[4,1024,1]{2,1,0:T(8,128)} %reshape.378.doc_col, f32[1024,128]{1,0:T(8,128)} %concatenate.68.cos, ...), custom_call_target="tpu_custom_call" | custom-call | tf_op jit(solution)/shard_map/attention/pallas_call | solution.py:724
  259.2 28.4 %exchange.3 = bf16[4,1024,256]{2,1,0:T(8,128)(2,1)} custom-call(bf16[4,1024,256]{2,1,0:T(8,128)(2,1)} %bitcast.139), custom_call_target="tpu_custom_call" | custom-call | tf_op jit(solution)/shard_map/exchange/pallas_call | solution.py:561
  287.6 3.4 slice_bitcast_fusion.2
  296.8 2.8 convert_reduce_fusion.1
  299.6 4.6 convert_reduce_fusion
  304.2 13.2 %fusion.37 = (f32[2048]{0:T(1024)S(1)}, f32[2048]{0:T(1024)S(1)}, bf16[1024,2048]{1,0:T(8,128)(2,1)}) fusion(f32[1024]{0:T(1024)S(1)} %rsqrt_bitcast_fusion, f32[1024]{0:T(1024)S(1)} %get-tuple-element.85, bf16[8,272,2048]{2,1,0:T(8,128)(2,1)} %get-tuple-element.51.xd, bf16[2048,1792]{1,0:T(8,128)(2,1)} %get-tuple-element.52.wc, ...), kind=kOutput, calls=%fused_computation.109 | convolution fusion | flops 7541878784 | bytes 19423232 | tf_op jit(solution)/shard_map/dot_general | solution.py:58
  319.2 2.7 slice.153
  322.2 7.8 %convolution_convert_fusion.dw2 = bf16[1280,2048]{1,0:T(8,128)(2,1)} fusion(bf16[1024,2048]{1,0:T(8,128)(2,1)S(1)} %bitcast.130, bf16[1024,256]{1,0:T(8,128)(2,1)S(1)} %copy.125, bf16[1024,1024]{1,0:T(8,128)(2,1)S(1)} %copy-done.17), kind=kOutput, calls=%fused_computation.7 | convolution fusion | flops 5376573440 | bytes 12058624 | tf_op jit(solution)/shard_map/dot_general | solution.py:52
  330.0 10.1 %convolution_convert_fusion.1.dw1 = bf16[2048,1792]{1,0:T(8,128)(2,1)} fusion(bf16[1024,2048]{1,0:T(8,128)(2,1)S(1)} %copy-done.16, bf16[1024,1024]{1,0:T(8,128)(2,1)S(1)} %copy-done.19, bf16[1024,256]{1,0:T(8,128)(2,1)S(1)} %copy-done.11, bf16[1024,512]{1,0:T(8,128)(2,1)S(1)} %copy.128), kind=kOutput, calls=%fused_computation.8 | convolution fusion | flops 7530872832 | bytes 15204352 | tf_op jit(solution)/shard_map/dot_general | solution.py:52
  340.1 7.1 %convolution_convert_fusion.2 = bf16[1024,2048]{1,0:T(8,128)(2,1)} fusion(bf16[1280,2048]{1,0:T(8,128)(2,1)S(1)} %bitcast.129, bf16[1024,256]{1,0:T(8,128)(2,1)S(1)} %copy-done.13, bf16[1024,1024]{1,0:T(8,128)(2,1)S(1)} %copy-done.17), kind=kOutput, calls=%fused_computation.10 | convolution fusion | flops 5376049152 | bytes 12058624 | tf_op jit(solution)/shard_map/dot_general | solution.py:994
  347.2 6.3 %pad_maximum_fusion.part = bf16[8,2,128,2048]{3,2,1,0:T(8,128)(2,1)} fusion(bf16[8,1,128,2048]{3,2,1,0:T(8,128)(2,1)S(1)} %bitcast.135, bf16[8,1,128,2048]{3,2,1,0:T(8,128)(2,1)} %bitcast.136), kind=kLoop, calls=%fused_computation | loop fusion | flops 4194304 | bytes 16777216 | tf_op jit(solution)/shard_map/stack | solution.py:1003
  353.5 150.3 %reduce_all.1 = (f32[2,128,2048]{2,1,0:T(8,128)}, bf16[8,64,1792]{2,1,0:T(8,128)(2,1)}, f32[320,2048]{1,0:T(8,128)}, f32[8,16,128]{2,1,0:T(8,128)}) custom-call(bf16[8,2,128,2048]{3,2,1,0:T(8,128)(2,1)} %pad_maximum_fusion.part, bf16[2048,1792]{1,0:T(8,128)(2,1)} %convolution_convert_fusion.1.dw1, bf16[1280,2048]{1,0:T(8,128)(2,1)} %convolution_convert_fusion.dw2, ...), custom_call_target="tpu_custom_call" | custom-call | tf_op jit(solution)/shard_map/reduce_all/pallas_call | solution.py:900
  505.8 2.2 slice.191
  507.9 3.0 reshape.361
  511.0 2.7 copy.155
  513.6 2.8 reshape.362
  525.9 2.9 copy.138
  528.8 2.1 reshape.371
  530.9 3.3 slice.174
  (185 shorter events, 58.5 us)
Async XLA Ops:
  13.1 3.4 copy-start.6
  15.7 4.5 copy-start.15
  16.5 1.6 copy-start.9
  16.6 3.7 copy-start.1
  16.6 3.7 copy-start.7
  20.2 130.0 %copy-start.20 = (s32[16]{0:T(128)S(1)}, s32[16]{0:T(128)}, u32[]{:S(2)}) copy-start(s32[16]{0:T(128)} %param.21) | copy-start | bytes 196
  287.6 5.9 %copy-start = (bf16[4,1024,256]{2,1,0:T(8,128)(2,1)S(1)}, bf16[4,1024,256]{2,1,0:T(8,128)(2,1)}, u32[]{:S(2)}) copy-start(bf16[4,1024,256]{2,1,0:T(8,128)(2,1)} %exchange.3) | copy-start | bytes 6291460
  299.6 4.6 copy-start.10
  299.6 4.6 copy-start.18
  304.2 14.4 %copy-start.4 = (bf16[1024,4,64]{2,0,1:T(8,128)(2,1)S(1)}, bf16[1024,4,64]{2,0,1:T(8,128)(2,1)}, u32[]{:S(2)}) copy-start(bf16[1024,4,64]{2,0,1:T(8,128)(2,1)} %get-tuple-element.77) | copy-start | bytes 1572868
  319.1 2.8 copy-start.12
  319.1 3.0 copy-start.17
  319.2 21.0 %slice-start = ((s8[5242880]{0:T(1024)(128)(4,1)}), s8[4194304]{0:T(1024)(128)(4,1)S(1)}, s32[]{:S(2)}) async-start(s8[5242880]{0:T(1024)(128)(4,1)} %bitcast.128), calls=%async_computation | async-start | bytes 8388608
  322.2 7.8 %copy-start.11 = (bf16[1024,256]{1,0:T(8,128)(2,1)S(1)}, bf16[1024,256]{1,0:T(8,128)(2,1)}, u32[]{:S(2)}) copy-start(bf16[1024,256]{1,0:T(8,128)(2,1)} %copy.129) | copy-start | bytes 1572868
  322.2 7.8 %copy-start.16 = (bf16[1024,2048]{1,0:T(8,128)(2,1)S(1)}, bf16[1024,2048]{1,0:T(8,128)(2,1)}, u32[]{:S(2)}) copy-start(bf16[1024,2048]{1,0:T(8,128)(2,1)} %get-tuple-element.59) | copy-start | bytes 12582916
  322.2 7.8 %copy-start.19 = (bf16[1024,1024]{1,0:T(8,128)(2,1)S(1)}, bf16[1024,1024]{1,0:T(8,128)(2,1)}, u32[]{:S(2)}) copy-start(bf16[1024,1024]{1,0:T(8,128)(2,1)} %get-tuple-element.58) | copy-start | bytes 6291460
  322.2 17.9 %slice-start.1 = ((s8[5242880]{0:T(1024)(128)(4,1)}), s8[1048576]{0:T(1024)(128)(4,1)S(1)}, s32[]{:S(2)}) async-start(s8[5242880]{0:T(1024)(128)(4,1)} %bitcast.128), calls=%async_computation.1 | async-start | bytes 2097152
  330.0 10.1 %copy-start.13 = (bf16[1024,256]{1,0:T(8,128)(2,1)S(1)}, bf16[1024,256]{1,0:T(8,128)(2,1)}, u32[]{:S(2)}) copy-start(bf16[1024,256]{1,0:T(8,128)(2,1)} %copy-done.12) | copy-start | bytes 1572868
  340.1 7.1 %copy-start.5 = (bf16[1024,2048]{1,0:T(8,128)(2,1)S(1)}, bf16[1024,2048]{1,0:T(8,128)(2,1)}, u32[]{:S(2)}) copy-start(bf16[1024,2048]{1,0:T(8,128)(2,1)} %get-tuple-element.74) | copy-start | bytes 12582916
  521.5 2.1 copy-start.2
  530.9 3.8 copy-start.3
  530.9 3.8 copy-start.14
  530.9 4.1 copy-start.8
  540.0 0.5 copy-start.21

commit v2 on v1

--- a/solution.py
+++ b/solution.py
@@ -359,11 +359,9 @@
         flip, step = q // 4, q % 4
         return (self.yb if flip else self.y), lax.rem(self.z + 4 - step, 4)
 
-    def barrier(self, members=True, square=True):
+    def barrier(self, more=()):
         sem = pltpu.get_barrier_semaphore()
-        peers = [self.member(q)[0] for q in range(1, 8)] if members else []
-        if square:
-            peers += [self.to_x, self.to_c]
+        peers = [self.member(q)[0] for q in range(1, 8)] + [self.to_x, self.to_c, *more]
         for peer in peers:
             pl.semaphore_signal(sem, inc=1, device_id=peer, device_id_type=MESH)
         pl.semaphore_wait(sem, len(peers))
@@ -393,13 +391,39 @@
     pltpu.make_async_copy(like, like, recv).wait()
 
 
-PARTS = ((0, 128), (128, 144))
-
-
-def gather_kernel(xd, ws, es, w2, xdg, wc, eg, w2g, loc, us, ur, ds_, dr, ys, yr, as_, ar, es_, er,
-                  wxs, wxr, wks, wkr, exs, exr, eks, ekr, fxs, fxr, fks, fkr):
+def head_tiles(src, dst, rows):
+    qkv, ff = src
+    low = lanes_of((rows, 128)) < 64
+
+    def tile(base, h):
+        t = 128 * (h // 2)
+        return qkv[:, base + t : base + t + 128].astype(F32)
+
+    def join(a, b, odd):
+        if odd:
+            return jnp.where(low, pltpu.roll(a, 64, 1), b).astype(BF)
+        return jnp.where(low, a, pltpu.roll(b, 64, 1)).astype(BF)
+
+    for mm in range(8):
+        first = (mm // 4) * 16 + mm % 4
+        odd = first % 2
+        for g in range(4):
+            h = first + 4 * g
+            dst(mm, 128 * g, join(tile(0, h), tile(2048, h), odd))
+            dst(mm, 768 + 256 * g, ff[:, 256 * h : 256 * h + 256])
+        for k in range(2):
+            h = first + 8 * k
+            dst(mm, 512 + 128 * k, join(tile(4096, h), tile(4096, h + 4), odd))
+
+
+def gather_kernel(x, dy, docs, qkv, ff, qb, fb, small, fc2, dense, cos, sin,
+                  xg, dg, docg, normed_o, act_o, dup_o, wc_o, w2_o, heads, dsum, cst,
+                  xv, dv, wc, w2g, eg, ws, es, nrm, act, dup, hs,
+                  loc, us, ur, ds_, dr, ys, yr, as_, ar, es_, er,
+                  wxs, wxr, wks, wkr, exs, exr, eks, ekr, fxs, fxr, fks, fkr, hss, hsr, hl, wb):
     n = Net()
-    n.barrier()
+    far = {"ctx": n.ctx + 2 * (1 - 2 * n.x) + 1 - 2 * n.c, "fsdp": n.z}
+    n.barrier(more=(far,))
 
     def wrow(yy, xx, cc, zz):
         return wc.at[pl.ds(pl.multiple_of((yy * 16 + xx * 8 + cc * 4 + zz) * 64, 64), 64)]
@@ -410,55 +434,74 @@
     def thin(gg):
         return w2g.at[pl.ds(pl.multiple_of(1024 + gg * 64, 64), 64)]
 
-    def shard(zz, p):
-        return xdg.at[n.y * 4 + zz, pl.ds(*PARTS[p])]
-
-    for q in range(1, 8):
+    def shard(yy, zz, p):
+        mm = yy * 4 + zz
+        if p == 2:
+            return docg.at[mm]
+        return (xv, dv)[p].at[pl.ds(pl.multiple_of(mm * 128, 128), 128)]
+
+    mine = (x, dy, docs)
+    parts = (0, 1, 2)
+
+    def tokens(p):
+        n.go(remote(mine[p], shard(n.y, n.z, p), us.at[p, 0], ur.at[p, 0], n.up), n.z < 3)
+        n.go(remote(mine[p], shard(n.y, n.z, p), ds_.at[p, 0], dr.at[p, 0], n.dn), n.z > 0)
+        n.go(remote(mine[p], shard(n.y, n.z, p), ys.at[p, 0], yr.at[p, n.z], n.to_y))
+
+    tokens(0)
+    rows2 = ((fc2, wide), (dense, thin))
+    for k, (ref, part) in enumerate(rows2):
+        n.go(remote(ref, part(n.g), fxs.at[k], fxr.at[k], n.to_x))
+        n.go(remote(ref, part(n.g), fks.at[k], fkr.at[k], n.to_c))
+
+    def put_w(mm, col, value):
+        ws[mm, :, col : col + value.shape[1]] = value
+
+    def put_e(mm, col, value):
+        es[mm, 0:1, col : col + value.shape[1]] = value[0:1]
+
+    for mm in range(8):
+        es[mm] = small[...]
+    head_tiles((qkv, ff), put_w, 64)
+    head_tiles((qb, fb), put_e, 8)
+    for q in (4, 1, 3, 5, 7, 2, 6):
         to, yy, zz = n.member(q)
         n.go(remote(es.at[yy * 4 + zz], eg.at[n.g * 8 + n.m], es_.at[q], er.at[q], to))
         n.go(remote(ws.at[yy * 4 + zz], wrow(n.y, n.x, n.c, n.z), as_.at[q], ar.at[q], to))
-    for p in range(2):
-        rows = pl.ds(*PARTS[p])
-        n.go(remote(xd.at[rows], shard(n.z, p), us.at[p, 0], ur.at[p, 0], n.up), n.z < 3)
-        n.go(remote(xd.at[rows], shard(n.z, p), ds_.at[p, 0], dr.at[p, 0], n.dn), n.z > 0)
-        n.go(remote(xd.at[rows], shard(n.z, p), ys.at[p, 0], yr.at[p, 0], n.to_y))
-    halves = ((pl.ds(0, 256), wide), (pl.ds(256, 64), thin))
-    for k, (rows, part) in enumerate(halves):
-        n.go(remote(w2.at[rows], part(n.g), fxs.at[k], fxr.at[k], n.to_x))
-        n.go(remote(w2.at[rows], part(n.g), fks.at[k], fkr.at[k], n.to_c))
     own = ws.at[n.m]
     n.go(remote(own, wrow(n.y, n.x, n.c, n.z), wxs.at[0], wxr.at[0], n.to_x))
     n.go(remote(own, wrow(n.y, n.x, n.c, n.z), wks.at[0], wkr.at[0], n.to_c))
+    tokens(1)
+    tokens(2)
     local = [
-        pltpu.make_async_copy(xd, xdg.at[n.m], loc.at[0]),
-        pltpu.make_async_copy(own, wrow(n.y, n.x, n.c, n.z), loc.at[1]),
-        pltpu.make_async_copy(es.at[n.m], eg.at[n.g * 8 + n.m], loc.at[2]),
-        pltpu.make_async_copy(w2.at[pl.ds(0, 256)], wide(n.g), loc.at[3]),
-        pltpu.make_async_copy(w2.at[pl.ds(256, 64)], thin(n.g), loc.at[4]),
+        pltpu.make_async_copy(x, shard(n.y, n.z, 0), loc.at[0]),
+        pltpu.make_async_copy(dy, shard(n.y, n.z, 1), loc.at[1]),
+        pltpu.make_async_copy(docs, shard(n.y, n.z, 2), loc.at[2]),
+        pltpu.make_async_copy(own, wrow(n.y, n.x, n.c, n.z), loc.at[3]),
+        pltpu.make_async_copy(es.at[n.m], eg.at[n.g * 8 + n.m], loc.at[4]),
+        pltpu.make_async_copy(fc2, wide(n.g), loc.at[5]),
+        pltpu.make_async_copy(dense, thin(n.g), loc.at[6]),
     ]
     for copy in local:
         copy.start()
 
-    def line(d, p):
+    def line(d, ps):
         below, above = n.z >= d, n.z + d <= 3
-
-        @pl.when(below)
-        def _():
-            arrive(shard(n.z - d, p), ur.at[p, d - 1])
-
-        if d < 3:
-            n.go(remote(shard(n.z - d, p), shard(n.z - d, p), us.at[p, d], ur.at[p, d], n.up),
-                 below & (n.z < 3))
-        n.go(remote(shard(n.z - d, p), shard(n.z - d, p), ys.at[p, d], yr.at[p, d], n.to_y), below)
-
-        @pl.when(above)
-        def _():
-            arrive(shard(n.z + d, p), dr.at[p, d - 1])
-
-        if d < 3:
-            n.go(remote(shard(n.z + d, p), shard(n.z + d, p), ds_.at[p, d], dr.at[p, d], n.dn),
-                 above & (n.z > 0))
-        n.go(remote(shard(n.z + d, p), shard(n.z + d, p), ys.at[p, d + 3], yr.at[p, d + 3], n.to_y), above)
+        for p in ps:
+            for there, zz, recv, send, nxt, more, to in (
+                (below, n.z - d, ur, us, ur, n.z < 3, n.up),
+                (above, n.z + d, dr, ds_, dr, n.z > 0, n.dn),
+            ):
+                block = shard(n.y, zz, p)
+
+                @pl.when(there)
+                def _():
+                    arrive(block, recv.at[p, d - 1])
+
+                if d < 3:
+                    n.go(remote(block, block, send.at[p, d], nxt.at[p, d], to), there & more)
+                slot = d if to is n.up else d + 3
+                n.go(remote(block, block, ys.at[p, slot], yr.at[p, zz], n.to_y), there)
 
     def pieces(qs):
         for q in qs:
@@ -475,67 +518,160 @@
             arrive(block, wxr.at[q])
             n.go(remote(block, block, wks.at[8 + q], wkr.at[8 + q], n.to_c))
 
-    line(1, 0)
+    line(1, (0,))
     pieces((4, 1, 3))
-    line(1, 1)
+    line(1, (1, 2))
     pieces((5, 7, 2, 6))
     for q in range(1, 8):
         yy, zz = n.source(q)
         arrive(eg.at[n.g * 8 + yy * 4 + zz], er.at[q])
-    local[2].wait()
-    mine = eg.at[pl.ds(n.g * 8, 8)]
-    n.go(remote(mine, mine, exs.at[0], exr.at[0], n.to_x))
-    n.go(remote(mine, mine, eks.at[0], ekr.at[0], n.to_c))
-    line(2, 0)
-    line(2, 1)
+    local[4].wait()
+    these = eg.at[pl.ds(n.g * 8, 8)]
+    n.go(remote(these, these, exs.at[0], exr.at[0], n.to_x))
+    n.go(remote(these, these, eks.at[0], ekr.at[0], n.to_c))
+    line(2, parts)
     gx = n.xb * 2 + n.c
-    for k, (rows, part) in enumerate(halves):
+    for k, (ref, part) in enumerate(rows2):
         arrive(part(gx), fxr.at[k])
         n.go(remote(part(gx), part(gx), fks.at[2 + k], fkr.at[2 + k], n.to_c))
     theirs = eg.at[pl.ds(gx * 8, 8)]
-    relay((0, 4, 1, 3))
-    line(3, 0)
-    relay((5, 7, 2, 6))
+    relay((0, 4, 1, 3, 5, 7, 2, 6))
     arrive(theirs, exr.at[0])
     n.go(remote(theirs, theirs, eks.at[1], ekr.at[1], n.to_c))
-    line(3, 1)
+    line(3, parts)
     for q in range(8):
         yy, zz = n.source(q)
         arrive(wrow(yy, n.x, n.cb, zz), wkr.at[q])
         arrive(wrow(yy, n.xb, n.cb, zz), wkr.at[8 + q])
     for k in range(2):
-        arrive(eg.at[pl.ds((2 * (n.xb if k else n.x) + n.cb) * 8, 8)], ekr.at[k])
-        for j, (rows, part) in enumerate(halves):
-            arrive(part(2 * (n.xb if k else n.x) + n.cb), fkr.at[2 * k + j])
-    for p in range(2):
-        rows = pl.ds(*PARTS[p])
-        arrive(xdg.at[n.yb * 4 + n.z, rows], yr.at[p, 0])
-        for d in range(1, 4):
-            @pl.when(n.z >= d)
-            def _():
-                arrive(xdg.at[n.yb * 4 + n.z - d, rows], yr.at[p, d])
-
-            @pl.when(n.z + d <= 3)
-            def _():
-                arrive(xdg.at[n.yb * 4 + n.z + d, rows], yr.at[p, d + 3])
-    for k in (0, 1, 3, 4):
+        gg = 2 * (n.xb if k else n.x) + n.cb
+        arrive(eg.at[pl.ds(gg * 8, 8)], ekr.at[k])
+        for j, (ref, part) in enumerate(rows2):
+            arrive(part(gg), fkr.at[2 * k + j])
+    for k in (0, 1, 2, 3, 5, 6):
         local[k].wait()
+    out_w = [pltpu.make_async_copy(wc, wc_o, wb.at[0]), pltpu.make_async_copy(w2g, w2_o, wb.at[1])]
+    for copy in out_w:
+        copy.start()
+
+    def add_ext(i, t):
+        return t + eg[i].astype(F32)
+
+    ext = lax.fori_loop(0, 32, add_ext, jnp.zeros((8, 1792), F32))
+    cst[0:1, 0:1792], cst[0:1, 1792:2048] = ext[1:2], ext[5:6, 0:256]
+    cst[1:2, 0:1792], cst[1:2, 1792:2048] = ext[2:3], ext[5:6, 256:512]
+    cst[2:3, 0:1792], cst[2:3, 1792:2048] = ext[3:4] + ext[4:5], ext[5:6, 512:768] + ext[5:6, 768:1024]
+    cst[3:4, 0:1792], cst[3:4, 1792:2048] = ext[0:1], jnp.zeros((1, 256), F32)
+    cst[4:8, :] = jnp.zeros((4, 2048), F32)
+    dsum[...] = jnp.zeros_like(dsum)
+    z0 = lax.div(n.z, 2)
+    half = lanes_of((256, 128)) < 64
+
+    def rows_of(j):
+        yy = n.y + lax.div(j, 2) * (1 - 2 * n.y)
+        zp = z0 + lax.rem(j, 2) * (1 - 2 * z0)
+        return yy, zp, pl.ds(pl.multiple_of((yy * 4 + 2 * zp) * 128, 256), 256)
+
+    def sends(j):
+        yy, zp, rows = rows_of(j)
+        return [
+            remote(hs.at[gg, rows], heads.at[n.g, rows], hss.at[j, k], hsr.at[j, k], to)
+            for k, (to, gg) in enumerate(((far, 2 * n.xb + n.cb), (n.to_x, 2 * n.xb + n.c), (n.to_c, 2 * n.x + n.cb)))
+        ]
+
+    def keeps(j):
+        yy, zp, rows = rows_of(j)
+        return [
+            pltpu.make_async_copy(hs.at[n.g, rows], heads.at[n.g, rows], hl.at[j, 0]),
+            pltpu.make_async_copy(nrm.at[rows], normed_o.at[rows], hl.at[j, 1]),
+            pltpu.make_async_copy(act.at[rows], act_o.at[rows], hl.at[j, 2]),
+            pltpu.make_async_copy(dup.at[rows], dup_o.at[rows], hl.at[j, 3]),
+            pltpu.make_async_copy(xv.at[rows], xg.at[rows], hl.at[j, 4]),
+            pltpu.make_async_copy(dv.at[rows], dg.at[rows], hl.at[j, 5]),
+        ]
+
+    def pair(j, carry):
+        yy, zp, rows = rows_of(j)
+        base = (yy * 4 + 2 * zp) * 128
+
+        @pl.when(j >= 2)
+        def _():
+            for k in range(2):
+                for p in parts:
+                    arrive(shard(yy, 2 * zp + k, p), yr.at[p, 2 * zp + k])
+
+        def norm(i, c):
+            sl = pl.ds(pl.multiple_of(base + 32 * i, 32), 32)
+            xf = xv[sl, :].astype(F32)
+            cen = xf - jnp.mean(xf, axis=-1, keepdims=True)
+            rstd = lax.rsqrt(jnp.mean(cen * cen, axis=-1, keepdims=True) + EPS)
+            nrm[sl, :] = (cen * rstd * cst[0:1, :] + cst[1:2, :]).astype(BF)
+            return c
+
+        lax.fori_loop(0, 8, norm, 0)
+        table = pl.ds(pl.multiple_of(yy * 128, 128), 128)
+        cosv = jnp.concatenate([cos[table, :]] * 2, axis=0)
+        sinv = jnp.concatenate([sin[table, :]] * 2, axis=0)
+        for k in range(2):
+            t2 = jnp.dot(nrm[rows, :], wc[:, 256 * k : 256 * k + 256], preferred_element_type=F32)
+            t2 = t2 + cst[3:4, 256 * k : 256 * k + 256]
+            for i in range(2):
+                t = t2[:, 128 * i : 128 * i + 128]
+                hs[2 * k + i, rows, 0:128] = (t * cosv + partner(t) * sinv).astype(BF)
+        v4 = jnp.dot(nrm[rows, :], wc[:, 512:768], preferred_element_type=F32) + cst[3:4, 512:768]
+        d4 = dot_nt(dv[rows, :], w2g[1024:1280, :])
+        for g in range(4):
+            v, d = (t[:, 128 * (g // 2) : 128 * (g // 2) + 128] for t in (v4, d4))
+            if g % 2 == 0:
+                vd = jnp.where(half, v, pltpu.roll(d, 64, 1))
+            else:
+                vd = jnp.where(half, pltpu.roll(v, 64, 1), d)
+            hs[g, rows, 128:256] = vd.astype(BF)
+        for copy in sends(j):
+            copy.start()
+        for k in range(4):
+            cols, wcols = slice(256 * k, 256 * k + 256), slice(768 + 256 * k, 1024 + 256 * k)
+            up = jnp.dot(nrm[rows, :], wc[:, wcols], preferred_element_type=F32) + cst[3:4, wcols]
+            a, slope = gelu_pair(up)
+            act[rows, cols] = a.astype(BF)
+            du = dot_nt(dv[rows, :], w2g[cols, :]) * slope
+            dup[rows, cols] = du.astype(BF)
+            dsum[:, cols] += jnp.broadcast_to(jnp.sum(du, axis=0, keepdims=True), (8, 256))
+        for copy in keeps(j):
+            copy.start()
+        return carry
+
+    lax.fori_loop(0, 4, pair, 0)
+    for j in range(4):
+        for copy in sends(j):
+            copy.wait()
+        for copy in keeps(j):
+            copy.wait()
+    for copy in out_w:
+        copy.wait()
     n.drain()
 
 
-def gather_all(xd, ws, es, w2):
+def gather_all(x, dy, docs, qkv, ff, qb, fb, small, fc2, dense, cos, sin):
     sd = jax.ShapeDtypeStruct
+    V = pltpu.VMEM
     return pl.pallas_call(
         gather_kernel,
         name="gather_all",
-        out_shape=(sd((8, 272, 2048), BF), sd((2048, 1792), BF), sd((32, 8, 1792), BF), sd((1280, 2048), BF)),
-        in_specs=[VM] * 4,
-        out_specs=(HBM,) * 4,
-        scratch_shapes=[DMA((5,)), DMA((2, 3)), DMA((2, 3)), DMA((2, 3)), DMA((2, 3)), DMA((2, 7)), DMA((2, 7)),
+        out_shape=(sd((1024, 2048), BF), sd((1024, 2048), BF), sd((8, 8, 1024), BF), sd((1024, 2048), BF),
+                   sd((1024, 1024), BF), sd((1024, 1024), BF), sd((2048, 1792), BF), sd((1280, 2048), BF),
+                   sd((4, 1024, 256), BF), sd((8, 1024), F32), sd((8, 2048), F32)),
+        in_specs=[VM] * 12,
+        out_specs=(HBM, HBM, VM, HBM, HBM, HBM, HBM, HBM, HBM, VM, VM),
+        scratch_shapes=[V((1024, 2048), BF), V((1024, 2048), BF), V((2048, 1792), BF), V((1280, 2048), BF),
+                        V((32, 8, 1792), BF), V((8, 64, 1792), BF), V((8, 8, 1792), BF),
+                        V((1024, 2048), BF), V((1024, 1024), BF), V((1024, 1024), BF), V((4, 1024, 256), BF),
+                        DMA((7,)), DMA((3, 3)), DMA((3, 3)), DMA((3, 3)), DMA((3, 3)), DMA((3, 7)), DMA((3, 4)),
                         DMA((8,)), DMA((8,)), DMA((8,)), DMA((8,)), DMA((8,)), DMA((8,)), DMA((16,)), DMA((16,)),
-                        DMA((1,)), DMA((1,)), DMA((2,)), DMA((2,)), DMA((2,)), DMA((2,)), DMA((4,)), DMA((4,))],
+                        DMA((1,)), DMA((1,)), DMA((2,)), DMA((2,)), DMA((2,)), DMA((2,)), DMA((4,)), DMA((4,)),
+                        DMA((4, 3)), DMA((4, 3)), DMA((4, 6)), DMA((2,))],
         compiler_params=pltpu.CompilerParams(collective_id=1, has_side_effects=True, vmem_limit_bytes=VLIM),
-    )(xd, ws, es, w2)
+    )(x, dy, docs, qkv, ff, qb, fb, small, fc2, dense, cos, sin)
 
 
 def exchange_kernel(src, dst, loc, ss, rs):
@@ -586,81 +722,7 @@
     return lax.dot_general(a, b, (((0,), (0,)), ((), ())), preferred_element_type=F32)
 
 
-def project_kernel(xd, wc, w2, gain, bias, wbias, cos, sin, normed_o, qkvd_o, act_o, dup_o, dsum_o):
-    xf = xd[0, 0:128, :].astype(F32)
-    mean = jnp.mean(xf, axis=-1, keepdims=True)
-    cen = xf - mean
-    rstd = lax.rsqrt(jnp.mean(cen * cen, axis=-1, keepdims=True) + EPS)
-    normed = (cen * rstd * gain[...] + bias[...]).astype(BF)
-    normed_o[...] = normed
-    dy = xd[0, 128:256, :]
-    dd = dot_nt(dy, w2[1024:1280, :])
-    half = lanes_of((128, 128)) < 64
-    cosv, sinv = cos[0], sin[0]
-    proj = jnp.dot(normed, wc[:, 0:768], preferred_element_type=F32) + wbias[:, 0:768]
-    for g in range(4):
-        t = proj[:, 128 * g : 128 * g + 128]
-        qkvd_o[g, 0, :, 0:128] = (t * cosv + partner(t) * sinv).astype(BF)
-        v = proj[:, 512 + 128 * (g // 2) : 640 + 128 * (g // 2)]
-        d = dd[:, 128 * (g // 2) : 128 * (g // 2) + 128]
-        if g % 2 == 0:
-            vd = jnp.where(half, v, pltpu.roll(d, 64, 1))
-        else:
-            vd = jnp.where(half, pltpu.roll(v, 64, 1), d)
-        qkvd_o[g, 0, :, 128:256] = vd.astype(BF)
-    for k in range(4):
-        cols = slice(256 * k, 256 * k + 256)
-        up = jnp.dot(normed, wc[:, 768 + 256 * k : 1024 + 256 * k], preferred_element_type=F32)
-        act, slope = gelu_pair(up + wbias[:, 768 + 256 * k : 1024 + 256 * k])
-        act_o[:, cols] = act.astype(BF)
-        dup = dot_nt(dy, w2[256 * k : 256 * k + 256, :]) * slope
-        dup_o[:, cols] = dup.astype(BF)
-        dsum = jnp.broadcast_to(jnp.sum(dup, axis=0, keepdims=True), (8, 256))
-
-        @pl.when(pl.program_id(0) == 0)
-        def _():
-            dsum_o[:, cols] = dsum
-
-        @pl.when(pl.program_id(0) > 0)
-        def _():
-            dsum_o[:, cols] += dsum
-
-
-def project(xdg, wc, w2g, gain, bias, wbias, cos, sin):
-    sd = jax.ShapeDtypeStruct
-    one = pl.Buffered(1)
-
-    def whole(shape):
-        return pl.BlockSpec(shape, lambda i: (0,) * len(shape), pipeline_mode=one)
-
-    return pl.pallas_call(
-        project_kernel,
-        name="project",
-        grid=(8,),
-        out_shape=(sd((1024, 2048), BF), sd((4, 8, 128, 256), BF), sd((1024, 1024), BF), sd((1024, 1024), BF),
-                   sd((8, 1024), F32)),
-        in_specs=[
-            pl.BlockSpec((1, 272, 2048), lambda i: (i, 0, 0)),
-            whole((2048, 1792)),
-            whole((1280, 2048)),
-            whole((1, 2048)),
-            whole((1, 2048)),
-            whole((1, 1792)),
-            pl.BlockSpec((1, 128, 128), lambda i: (i // 4, 0, 0)),
-            pl.BlockSpec((1, 128, 128), lambda i: (i // 4, 0, 0)),
-        ],
-        out_specs=(
-            pl.BlockSpec((128, 2048), lambda i: (i, 0)),
-            pl.BlockSpec((4, 1, 128, 256), lambda i: (0, i, 0, 0)),
-            pl.BlockSpec((128, 1024), lambda i: (i, 0)),
-            pl.BlockSpec((128, 1024), lambda i: (i, 0)),
-            pl.BlockSpec((8, 1024), lambda i: (0, 0)),
-        ),
-        compiler_params=pltpu.CompilerParams(vmem_limit_bytes=VLIM),
-    )(xdg, wc, w2g, gain, bias, wbias, cos, sin)
-
-
-def attention_kernel(slot_of, a, doc_row, doc_col, cos, sin, out, sums, seq, att, dq, dk, dv):
+def attention_kernel(slot_of, a, docs, cos, sin, out, sums, seq, att, dq, dk, dv):
     def where_is(p):
         r = slot_of[p]
         ctx = lax.div(r, 2)
@@ -685,7 +747,8 @@
         s = dot_nt(qs, kk) * scale
         qpos = 256 * i + lax.broadcasted_iota(jnp.int32, (256, kn), 0)
         kpos = k0 + lax.broadcasted_iota(jnp.int32, (256, kn), 1)
-        mask = (kpos <= qpos) & (doc_row[0, :, rk] == doc_col[0, rq, :])
+        own = jnp.broadcast_to(docs[0, 0:1, rq].astype(F32), (128, 256)).T[:, 0:1]
+        mask = (kpos <= qpos) & (docs[0, 0:1, rk].astype(F32) == own)
         s = jnp.where(mask, s, NEG)
         top = jnp.max(s, axis=-1, keepdims=True)
         e = jnp.where(mask, jnp.exp(s - top), 0.0)
@@ -729,8 +792,7 @@
             grid=(4,),
             in_specs=[
                 blk,
-                pl.BlockSpec((1, 1, 1024), lambda s, t: (s, 0, 0)),
-                pl.BlockSpec((1, 1024, 1), lambda s, t: (s, 0, 0)),
+                pl.BlockSpec((1, 8, 1024), lambda s, t: (s, 0, 0)),
                 pl.BlockSpec((1024, 128), lambda s, t: (0, 0)),
                 pl.BlockSpec((1024, 128), lambda s, t: (0, 0)),
             ],
@@ -739,7 +801,7 @@
         ),
         out_shape=(sd((4, 2, 4, 128, 256), BF), sd((4, 8, 256), F32)),
         compiler_params=pltpu.CompilerParams(vmem_limit_bytes=VLIM),
-    )(slot_of, a, docs[:, None, :], docs[:, :, None], cos, sin)
+    )(slot_of, a, docs, cos, sin)
 
 
 def add_rows(dst, srcs, rows, out=None, step=16):
@@ -936,14 +998,12 @@
 
 
 def rotary_lanes(pos):
-    half = ROT // 2
-    freqs = jnp.exp(-(2.0 * jnp.arange(half, dtype=F32) / ROT) * math.log(10000.0))
-    angles = pos.astype(F32)[..., None] * freqs
-    c, s = jnp.cos(angles), jnp.sin(angles)
-    one = jnp.ones(pos.shape + (32,), F32)
-    cos = jnp.concatenate([c, c, one] * 2, axis=-1)
-    sin = jnp.concatenate([-s, s, 0.0 * one] * 2, axis=-1)
-    return cos, sin
+    lane = jnp.arange(128, dtype=jnp.int32) % 64
+    freqs = jnp.exp(-(2.0 * (lane % (ROT // 2)).astype(F32) / ROT) * math.log(10000.0))
+    angles = pos.astype(F32)[:, None] * freqs[None]
+    turns = lane < ROT
+    sign = jnp.where(turns, jnp.where(lane < ROT // 2, -1.0, 1.0), 0.0)
+    return jnp.where(turns, jnp.cos(angles), 1.0), jnp.sin(angles) * sign
 
 
 def fast_device(
@@ -954,35 +1014,27 @@
     index = ctx * 4 + z
     xb, dyb = block_input[0], output_grad[0]
 
-    docs = jnp.zeros((16, 2048), BF).at[0, :1024].set(segment[0].astype(BF))
-    xd = jnp.concatenate([xb, dyb, docs], axis=0)
-    ws = member_columns(qkv_w, fc1_w)
-
     def spread(piece, total):
-        return lax.dynamic_update_slice(jnp.zeros((total,), BF), piece, (index * piece.shape[0],))
-
-    wb = member_columns(spread(qkv_b, 6144)[None], spread(fc1_b, 8192)[None])
-    small = jnp.stack([spread(v, 2048) for v in (ln_gain, ln_bias, dense_b, fc2_b)])
-    rest = jnp.zeros((1792,), BF).at[:1024].set(small[:, 1792:].reshape(1024))
-    es = jnp.concatenate([jnp.concatenate([small[:, :1792], rest[None], jnp.zeros((2, 1792), BF)])[None]] * 8)
-    es = jnp.concatenate([wb, es], axis=1)
-    w2 = jnp.concatenate([fc2_w, dense_w], axis=0)
-    xdg, wc, eg, w2g = gather_all(xd, ws, es, w2)
-
-    ext = jnp.sum(eg.astype(F32), axis=0)
-    wbias = ext[0:1]
-    vecs = jnp.concatenate([ext[1:5], ext[5, :1024].reshape(4, 256)], axis=1)
-    gain, lnb, ob = vecs[0:1], vecs[1:2], vecs[2:3] + vecs[3:4]
-    pos_of_row = slots[:, None] * 64 + jnp.arange(64, dtype=jnp.int32)[None]
-    rows2 = lax.dynamic_slice_in_dim(pos_of_row.reshape(2, 4, 128), g, 1, 1).reshape(2, 128)
-    cos, sin = rotary_lanes(rows2)
-    normed, qkvd, act, dup, dsum = project(xdg, wc, w2g, gain, lnb, wbias, cos, sin)
-
-    heads_in = exchange(qkvd.reshape(4, 1024, 256), 2)
+        count = piece.shape[0]
+        own = jnp.arange(total, dtype=jnp.int32) // count == index
+        return jnp.where(own, jnp.tile(piece, total // count), jnp.zeros((), BF))
+
+    docs = jnp.broadcast_to(segment.astype(BF), (8, 1024))
+    qb = jnp.broadcast_to(spread(qkv_b, 6144)[None], (8, 6144))
+    fb = jnp.broadcast_to(spread(fc1_b, 8192)[None], (8, 8192))
+    vecs = jnp.stack([spread(v, 2048) for v in (ln_gain, ln_bias, dense_b, fc2_b)])
+    rest = jnp.pad(vecs[:, 1792:].reshape(1, 1024), ((0, 0), (0, 768)))
+    small = jnp.concatenate([jnp.zeros((1, 1792), BF), vecs[:, :1792], rest, jnp.zeros((2, 1792), BF)], axis=0)
+    pairs = lax.dynamic_slice_in_dim(slots.reshape(2, 4, 2), g, 1, 1).reshape(4)
+    rows = (pairs[:, None] * 64 + jnp.arange(64, dtype=jnp.int32)[None]).reshape(256)
+    cos2, sin2 = rotary_lanes(rows)
+    cos, sin = rotary_lanes(jnp.arange(1024, dtype=jnp.int32))
+    xg, dg, docg, normed, act, dup, wc, w2g, heads, dsum, cst = gather_all(
+        xb, dyb, docs, qkv_w, fc1_w, qb, fb, small, fc2_w, dense_w, cos2, sin2
+    )
+    gain, ob = cst[0:1], cst[2:3]
     slot_of = jnp.sum(jnp.where(slots[None, :] == jnp.arange(16, dtype=jnp.int32)[:, None], jnp.arange(16, dtype=jnp.int32)[None, :], 0), axis=1)
-    cosp, sinp = rotary_lanes(jnp.arange(1024, dtype=jnp.int32))
-    docs4 = xdg[0:4, 256, 0:1024].astype(F32)
-    att, sums = attention(slot_of, heads_in.reshape(4, 2, 4, 128, 256), docs4, cosp, sinp)
+    att, sums = attention(slot_of, heads.reshape(4, 2, 4, 128, 256), docg, cos, sin)
     back = exchange(att.reshape(4, 1024, 256), 4)
 
     dqk = back[:, :, 0:128].transpose(1, 0, 2).reshape(1024, 512)
@@ -990,10 +1042,10 @@
     attn = back[:, :, 192:256].transpose(1, 0, 2).reshape(1024, 256)
     dpr = jnp.concatenate([dqk, dvv, dup], axis=1)
     up2 = jnp.concatenate([act, attn], axis=1)
-    dy_all = xdg[:, 128:256].reshape(1024, 2048)
+    dy_all = dg
     ypart = jnp.dot(up2, w2g, preferred_element_type=F32)
     dn = contract_cols(dpr, wc)
-    xf = xdg[:, 0:128].reshape(1024, 2048).astype(F32)
+    xf = xg.astype(F32)
     cen = xf - jnp.mean(xf, axis=-1, keepdims=True)
     xhat = cen * lax.rsqrt(jnp.mean(cen * cen, axis=-1, keepdims=True) + EPS)
     gpart = jnp.sum(dn * xhat, axis=0)

time: 550 us -> 461 us (0.84)
  Pallas kernels: 399 us -> 334 us
  local copies, waits for them, and re-layouts: 71.2 us -> 47.4 us
  matrix products: 38.2 us -> 44.1 us
    pallas_call x2 -> x1, Pallas kernels: 170 us -> 134 us  [gather_all(): pl.pallas_call(gather_kernel, name='gather_all', out_shape=(sd((1024, 204...]
    pallas_call x2 -> x1, Pallas kernels: 56.9 us -> 28.7 us  [exchange(): pl.pallas_call(exchange_kernel, name='exchange', out_shape=jax.ShapeDtype...]
    reshape x9 -> x1, local copies, waits for them, and re-layouts: 7.45 us -> 0.74 us  [fast_device(): pairs = lax.dynamic_slice_in_dim(slots.reshape(2, 4, 2), g, 1, 1).reshape(4)]
where the time goes in v2:
time: 461 us; the launch traced here: 453 us
  Pallas kernels  334 us (72%)
  local copies, waits for them, and re-layouts  47.4 us (10%)
  matrix products  44.1 us (10%)
  other arithmetic  26.7 us (6%)
    pallas_call x1, Pallas kernels, reduce_all(): pl.pallas_call(reduce_kernel, name='reduce_all', out_shape=(sd((2, 128, 2...  146 us
    pallas_call x1, Pallas kernels, gather_all(): pl.pallas_call(gather_kernel, name='gather_all', out_shape=(sd((1024, 204...  134 us
    pallas_call x1, Pallas kernels, exchange(): pl.pallas_call(exchange_kernel, name='exchange', out_shape=jax.ShapeDtype...  28.7 us
    pallas_call x1, Pallas kernels, attention(): pl.pallas_call(attention_kernel, name='attention', grid_spec=pltpu.Prefet...  24.3 us
    dot_general x2, matrix products, contract_rows(): lax.dot_general(left, right, (((0,), (0,)), ((), ())), preferred_element_...  20.2 us
    dot_general x1, matrix products, contract_cols(): lax.dot_general(left, right, (((1,), (1,)), ((), ())), preferred_element_...  13.6 us
    dot_general x1, matrix products, fast_device(): ypart = jnp.dot(up2, w2g, preferred_element_type=F32)  10.3 us

profile of v2, /device:TPU:8, one launch (start us, length us, event | category | flops | bytes accessed | tf_op | source)
XLA Modules:
  0.0 453.4 jit_solution(11850759112179308960)
XLA Ops:
  10.4 134.4 %gather_all.1 = (bf16[1024,2048]{1,0:T(8,128)(2,1)}, bf16[1024,2048]{1,0:T(8,128)(2,1)}, bf16[8,8,1024]{2,1,0:T(8,128)(2,1)}, bf16[1024,2048]{1,0:T(8,128)(2,1)}...) custom-call(bf16[128,2048]{1,0:T(8,128)(2,1)} %bitcast.82, ...), custom_call_target="tpu_custom_call" | custom-call | tf_op jit(solution)/shard_map/gather_all/pallas_call | solution.py:658
  144.8 3.0 convert_reduce_fusion
  150.1 3.1 fusion.20
  153.2 24.3 %attention.1 = (bf16[4,2,4,128,256]{4,3,2,1,0:T(8,128)(2,1)}, f32[4,8,256]{2,1,0:T(8,128)}) custom-call(s32[16]{0:T(128)} %select_reduce_fusion.slot_of, bf16[4,2,4,128,256]{4,3,2,1,0:T(8,128)(2,1)} %bitcast.91, bf16[8,8,1024]{2,1,0:T(8,128)(2,1)} %get-tuple-element.31.docs, f32[1024,128]{1,0:T(8,128)} %get-tuple-element.60.cos, ...), custom_call_target="tpu_custom_call" | custom-call | tf_op jit(solution)/shard_map/attention/pallas_call | solution.py:787
  177.4 28.7 %exchange.1 = bf16[4,1024,256]{2,1,0:T(8,128)(2,1)} custom-call(bf16[4,1024,256]{2,1,0:T(8,128)(2,1)} %bitcast.92), custom_call_target="tpu_custom_call" | custom-call | tf_op jit(solution)/shard_map/exchange/pallas_call | solution.py:697
  206.2 3.0 slice_bitcast_fusion.2
  210.4 2.0 copy.60
  213.7 13.6 %fusion.49 = (f32[2048]{0:T(1024)S(1)}, f32[2048]{0:T(1024)S(1)}, bf16[1024,2048]{1,0:T(8,128)(2,1)}) fusion(f32[1024]{0:T(1024)S(1)} %add_rsqrt_fusion, f32[1024]{0:T(1024)S(1)} %broadcast_multiply_fusion, bf16[1024,2048]{1,0:T(8,128)(2,1)} %get-tuple-element.40, bf16[2048,1792]{1,0:T(8,128)(2,1)} %get-tuple-element.35, ...), kind=kOutput, calls=%fused_computation.124 | convolution fusion | flops 7541878784 | bytes 19423232 | tf_op jit(solution)/shard_map/dot_general | solution.py:58
  228.0 10.3 %convolution_convert_fusion.2 = bf16[1024,2048]{1,0:T(8,128)(2,1)} fusion(bf16[1280,2048]{1,0:T(8,128)(2,1)} %get-tuple-element.33, bf16[1024,256]{1,0:T(8,128)(2,1)S(1)} %copy.56, bf16[1024,1024]{1,0:T(8,128)(2,1)} %get-tuple-element.29), kind=kOutput, calls=%fused_computation.11 | convolution fusion | flops 5376049152 | bytes 12058624 | tf_op jit(solution)/shard_map/dot_general | solution.py:1046
  238.3 6.2 %pad_maximum_fusion.part = bf16[8,2,128,2048]{3,2,1,0:T(8,128)(2,1)} fusion(bf16[8,1,128,2048]{3,2,1,0:T(8,128)(2,1)S(1)} %bitcast.87, bf16[8,1,128,2048]{3,2,1,0:T(8,128)(2,1)} %bitcast.88), kind=kLoop, calls=%fused_computation.7 | loop fusion | flops 4194304 | bytes 16777216 | tf_op jit(solution)/shard_map/stack | solution.py:1055
  244.5 12.5 %convolution_convert_fusion.1.dw1 = bf16[2048,1792]{1,0:T(8,128)(2,1)} fusion(bf16[1024,2048]{1,0:T(8,128)(2,1)} %get-tuple-element.36, bf16[1024,1024]{1,0:T(8,128)(2,1)} %get-tuple-element.34, bf16[1024,256]{1,0:T(8,128)(2,1)S(1)} %copy-done.12, bf16[1024,512]{1,0:T(8,128)(2,1)S(1)} %copy.59), kind=kOutput, calls=%fused_computation.10 | convolution fusion | flops 7530872832 | bytes 15204352 | tf_op jit(solution)/shard_map/dot_general | solution.py:52
  257.0 7.7 %convolution_convert_fusion.dw2 = bf16[1280,2048]{1,0:T(8,128)(2,1)} fusion(bf16[1024,2048]{1,0:T(8,128)(2,1)S(1)} %copy-done.6, bf16[1024,256]{1,0:T(8,128)(2,1)S(1)} %copy.56, bf16[1024,1024]{1,0:T(8,128)(2,1)S(1)} %copy-done.15), kind=kOutput, calls=%fused_computation.9 | convolution fusion | flops 5376573440 | bytes 12058624 | tf_op jit(solution)/shard_map/dot_general | solution.py:52
  266.6 2.8 convert_reduce_fusion.1
  270.4 146.1 %reduce_all.1 = (f32[2,128,2048]{2,1,0:T(8,128)}, bf16[8,64,1792]{2,1,0:T(8,128)(2,1)}, f32[320,2048]{1,0:T(8,128)}, f32[8,16,128]{2,1,0:T(8,128)}) custom-call(bf16[8,2,128,2048]{3,2,1,0:T(8,128)(2,1)} %pad_maximum_fusion.part, bf16[2048,1792]{1,0:T(8,128)(2,1)} %convolution_convert_fusion.1.dw1, bf16[1280,2048]{1,0:T(8,128)(2,1)} %convolution_convert_fusion.dw2, ...), custom_call_target="tpu_custom_call" | custom-call | tf_op jit(solution)/shard_map/reduce_all/pallas_call | solution.py:962
  419.7 3.3 fusion.17
  424.1 1.6 copy.83
  425.8 2.8 reshape.386
  430.2 2.7 copy.82
  432.9 2.8 reshape.384
  438.2 1.9 slice.95
  441.5 2.0 reshape.392
  443.5 3.0 copy.69
  446.5 2.1 reshape.393
  449.3 3.1 slice.99
  (134 shorter events, 28.8 us)
Async XLA Ops:
  0.6 2.8 copy-start
  144.8 3.5 copy-start.2
  144.8 4.7 %copy-start.14 = (s32[16]{0:T(128)S(1)}, s32[16]{0:T(128)}, u32[]{:S(2)}) copy-start(s32[16]{0:T(128)} %param.17) | copy-start | bytes 196
  206.2 6.3 %copy-start.3 = (bf16[4,1024,256]{2,1,0:T(8,128)(2,1)S(1)}, bf16[4,1024,256]{2,1,0:T(8,128)(2,1)}, u32[]{:S(2)}) copy-start(bf16[4,1024,256]{2,1,0:T(8,128)(2,1)} %exchange.1) | copy-start | bytes 6291460
  212.6 1.1 copy-start.11
  213.7 13.7 %copy-start.7 = (bf16[1024,4,64]{2,0,1:T(8,128)(2,1)S(1)}, bf16[1024,4,64]{2,0,1:T(8,128)(2,1)}, u32[]{:S(2)}) copy-start(bf16[1024,4,64]{2,0,1:T(8,128)(2,1)} %get-tuple-element.55) | copy-start | bytes 1572868
  228.0 10.3 %copy-start.8 = (bf16[1024,2048]{1,0:T(8,128)(2,1)S(1)}, bf16[1024,2048]{1,0:T(8,128)(2,1)}, u32[]{:S(2)}) copy-start(bf16[1024,2048]{1,0:T(8,128)(2,1)} %get-tuple-element.52) | copy-start | bytes 12582916
  238.3 6.2 %copy-start.12 = (bf16[1024,256]{1,0:T(8,128)(2,1)S(1)}, bf16[1024,256]{1,0:T(8,128)(2,1)}, u32[]{:S(2)}) copy-start(bf16[1024,256]{1,0:T(8,128)(2,1)} %copy.60) | copy-start | bytes 1572868
  244.5 12.5 %copy-start.6 = (bf16[1024,2048]{1,0:T(8,128)(2,1)S(1)}, bf16[1024,2048]{1,0:T(8,128)(2,1)}, u32[]{:S(2)}) copy-start(bf16[1024,2048]{1,0:T(8,128)(2,1)} %get-tuple-element.37) | copy-start | bytes 12582916
  244.5 12.5 %copy-start.15 = (bf16[1024,1024]{1,0:T(8,128)(2,1)S(1)}, bf16[1024,1024]{1,0:T(8,128)(2,1)}, u32[]{:S(2)}) copy-start(bf16[1024,1024]{1,0:T(8,128)(2,1)} %get-tuple-element.29) | copy-start | bytes 6291460
  270.4 147.2 %copy-start.4 = (bf16[1,128,2048]{2,1,0:T(8,128)(2,1)S(1)}, bf16[1,128,2048]{2,1,0:T(8,128)(2,1)}, u32[]{:S(2)}) copy-start(bf16[1,128,2048]{2,1,0:T(8,128)(2,1)} %param.14) | copy-start | bytes 1572868
  270.4 149.3 %copy-start.10 = (bf16[1,128,2048]{2,1,0:T(8,128)(2,1)S(1)}, bf16[1,128,2048]{2,1,0:T(8,128)(2,1)}, u32[]{:S(2)}) copy-start(bf16[1,128,2048]{2,1,0:T(8,128)(2,1)} %param.15) | copy-start | bytes 1572868
  416.5 6.4 %copy-start.13 = (f32[8,16,128]{2,1,0:T(8,128)S(1)}, f32[8,16,128]{2,1,0:T(8,128)}, u32[]{:S(2)}) copy-start(f32[8,16,128]{2,1,0:T(8,128)} %get-tuple-element.43) | copy-start | bytes 196612
  416.5 7.1 %copy-start.5 = (bf16[8,64,1792]{2,1,0:T(8,128)(2,1)S(1)}, bf16[8,64,1792]{2,1,0:T(8,128)(2,1)}, u32[]{:S(2)}) copy-start(bf16[8,64,1792]{2,1,0:T(8,128)(2,1)} %get-tuple-element.44) | copy-start | bytes 5505028
  430.2 5.5 %copy-start.9 = (f32[64,1,2048]{2,0,1:T(8,128)S(1)}, f32[64,1,2048]{2,0,1:T(8,128)}, u32[]{:S(2)}) copy-start(f32[64,1,2048]{2,0,1:T(8,128)} %reshape.386) | copy-start | bytes 1572868
  440.1 12.4 %copy-start.16 = (f32[64]{0:T(128)}, f32[64]{0:T(128)S(1)}, u32[]{:S(2)}) copy-start(f32[64]{0:T(128)S(1)} %slice_bitcast_fusion.4) | copy-start | bytes 772
  443.5 9.4 %copy-start.1 = (bf16[256]{0:T(256)(128)(2,1)S(1)}, bf16[256]{0:T(256)(128)(2,1)}, u32[]{:S(2)}) copy-start(bf16[256]{0:T(256)(128)(2,1)} %param.25) | copy-start | bytes 1540
